TPU v7x, 32 devices: a 4x4x1 block of a 4x4x8 slice. The times are simulated.
32 devices in a mesh: part: 1 (over z), tp: 4 (over y), ep: 8 (over x, core).
Axes of the slice: x: 4, y: 4, z: 1, core: 2. Of those that a mesh axis runs over, the one named last changes fastest.
The devices are a block of a 4x4x8 slice.
Arguments:
- dec_states: bfloat16 [64, 256, 768], P(('part', 'ep'))
- enc_states: bfloat16 [64, 128, 768], P(('part', 'ep'))
- enc_pad: int32 [64, 128], P(('part', 'ep'))
- expert_idx: int32 [64, 256], P(('part', 'ep'))
- self_bias: float32 [12, 256, 256], P('tp')
- gain_self: float32 [768], replicated
- wq_self: bfloat16 [768, 768], P(None, 'tp')
- wk_self: bfloat16 [768, 768], P(None, 'tp')
- wv_self: bfloat16 [768, 768], P(None, 'tp')
- wo_self: bfloat16 [768, 768], P('tp')
- gain_cross: float32 [768], replicated
- wq_cross: bfloat16 [768, 768], P(None, 'tp')
- wk_cross: bfloat16 [768, 768], P(None, 'tp')
- wv_cross: bfloat16 [768, 768], P(None, 'tp')
- wo_cross: bfloat16 [768, 768], P('tp')
- gain_ffn: float32 [768], replicated
- w_router: float32 [768, 32], replicated
- w_in: bfloat16 [32, 768, 3072], P('ep')
- w_out: bfloat16 [32, 3072, 768], P('ep')
Outputs:
- output: bfloat16 [64, 256, 768], P(('part', 'ep'))
All inputs are finite; a program needn't handle non-finite values.
Results may differ from a plain program's by a relative error of at most 0.0193591.
Values are sent between devices in bfloat16 or wider.
A program may use at most 768 MiB of HBM per device.

v0:
```python
import jax
import jax.numpy as jnp
from jax import lax
from jax.sharding import PartitionSpec as P

EPSILON = 1e-6
NEG_LARGE = -1e30


def rms_norm(states, gain_vec):
    upcast = states.astype(jnp.float32)
    mean_sq = jnp.mean(upcast * upcast, axis=-1, keepdims=True)
    return (upcast * lax.rsqrt(mean_sq + EPSILON) * gain_vec).astype(jnp.bfloat16)


def head_project(states, weight, heads):
    projected = jnp.einsum('bld,dk->blk', states, weight, preferred_element_type=jnp.float32)
    return projected.astype(jnp.bfloat16).reshape(states.shape[0], states.shape[1], heads, weight.shape[1] // heads)


def attention_heads(normed, source, bias_mask, w_query, w_key, w_value, w_output, heads):
    queries = head_project(normed, w_query, heads)
    key_heads = head_project(source, w_key, heads)
    values = head_project(source, w_value, heads)
    scores = jnp.einsum('bqhe,bkhe->bhqk', queries, key_heads, preferred_element_type=jnp.float32) + bias_mask
    weights = jax.nn.softmax(scores, axis=-1).astype(jnp.bfloat16)
    context = jnp.einsum('bhqk,bkhe->bhqe', weights, values, preferred_element_type=jnp.float32).astype(jnp.bfloat16)
    w_heads = w_output.reshape(heads, w_output.shape[0] // heads, w_output.shape[1])
    return jnp.einsum('cirf,ife->cre', context, w_heads, preferred_element_type=jnp.float32)


def router_choice(normed, choice, w_router):
    tokens, experts = normed.shape[0], w_router.shape[1]
    logits = jnp.dot(normed, w_router, precision=lax.Precision.HIGHEST, preferred_element_type=jnp.float32)
    router_prob = jax.nn.softmax(logits, axis=-1)
    one_hot = (choice[:, None] == lax.broadcasted_iota(jnp.int32, (tokens, experts), 1)).astype(jnp.int32)
    gate_prob = jnp.sum(router_prob * one_hot, axis=-1)
    position = jnp.sum((jnp.cumsum(one_hot, axis=0) - 1) * one_hot, axis=-1)
    return gate_prob, position


def expert_layer(states, expert_idx, gain_ffn, w_router, w_in, w_out, ep_size):
    batch_dev, dec_len, d_model = states.shape
    tokens = batch_dev * dec_len
    experts = w_router.shape[1]
    capacity = (5 * tokens + 4 * experts - 1) // (4 * experts)
    normed = rms_norm(states, gain_ffn).reshape(tokens, d_model)
    choice = expert_idx.reshape(tokens)
    gate_prob, position = router_choice(normed, choice, w_router)
    slot_id = jnp.where(position < capacity, choice * capacity + position, -1)
    dispatch = (slot_id[:, None] == lax.broadcasted_iota(jnp.int32, (tokens, experts * capacity), 1)).astype(jnp.bfloat16)
    send_buf = jnp.einsum('sc,sd->cd', dispatch, normed, preferred_element_type=jnp.float32).astype(jnp.bfloat16)
    received = lax.all_to_all(send_buf.reshape(experts, capacity, d_model), 'ep', 0, 0, tiled=True)
    received = received.reshape(ep_size, experts // ep_size, capacity, d_model)
    hidden = jnp.maximum(jnp.einsum('gecd,edf->gecf', received, w_in, preferred_element_type=jnp.float32), 0.0).astype(jnp.bfloat16)
    expert_out = jnp.einsum('gecf,efd->gecd', hidden, w_out, preferred_element_type=jnp.float32).astype(jnp.bfloat16)
    returned = lax.all_to_all(expert_out.reshape(experts, capacity, d_model), 'ep', 0, 0, tiled=True)
    combined = jnp.einsum('sc,cd->sd', dispatch, returned.reshape(experts * capacity, d_model), preferred_element_type=jnp.float32)
    result = states.reshape(tokens, d_model).astype(jnp.float32) + gate_prob[:, None] * combined
    return result.astype(jnp.bfloat16).reshape(batch_dev, dec_len, d_model)


def solution(mesh):
    ep_size = mesh.shape['ep']
    token_spec = P(('part', 'ep'), None, None)
    row_spec = P(('part', 'ep'), None)
    col_spec = P(None, 'tp')
    head_rows = P('tp', None)
    vec_spec = P(None)
    expert_spec = P('ep', None, None)
    in_specs = (token_spec, token_spec, row_spec, row_spec, P('tp', None, None), vec_spec, col_spec, col_spec, col_spec, head_rows, vec_spec, col_spec, col_spec, col_spec, head_rows, vec_spec, P(None, None), expert_spec, expert_spec)

    def layer(dec_states, enc_states, enc_pad, expert_idx, self_bias, gain_self, wq_self, wk_self, wv_self, wo_self, gain_cross, wq_cross, wk_cross, wv_cross, wo_cross, gain_ffn, w_router, w_in, w_out):
        dec_len = dec_states.shape[1]
        local_heads = self_bias.shape[0]
        row_ids = lax.broadcasted_iota(jnp.int32, (dec_len, dec_len), 0)
        col_ids = lax.broadcasted_iota(jnp.int32, (dec_len, dec_len), 1)
        causal_bias = jnp.where(col_ids <= row_ids, self_bias, NEG_LARGE)[None]
        normed = rms_norm(dec_states, gain_self)
        partial = attention_heads(normed, normed, causal_bias, wq_self, wk_self, wv_self, wo_self, local_heads)
        attn_sum = lax.psum(partial.astype(jnp.bfloat16), 'tp')
        after_self = (dec_states.astype(jnp.float32) + attn_sum.astype(jnp.float32)).astype(jnp.bfloat16)
        pad_bias = jnp.where(enc_pad == 0, 0.0, NEG_LARGE).astype(jnp.float32)[:, None, None, :]
        normed = rms_norm(after_self, gain_cross)
        partial = attention_heads(normed, enc_states, pad_bias, wq_cross, wk_cross, wv_cross, wo_cross, local_heads)
        attn_sum = lax.psum(partial.astype(jnp.bfloat16), 'tp')
        after_cross = (after_self.astype(jnp.float32) + attn_sum.astype(jnp.float32)).astype(jnp.bfloat16)
        return expert_layer(after_cross, expert_idx, gain_ffn, w_router, w_in, w_out, ep_size)

    return jax.shard_map(layer, mesh=mesh, in_specs=in_specs, out_specs=token_spec, check_vma=False)
```

profile of v0, /device:TPU:97, one launch (start us, length us, event | category | flops | bytes accessed | tf_op | source)
XLA Modules:
  0.0 382.1 jit_solution(9221785972993720365)
XLA Ops:
  6.5 0.0 copy-start
  6.6 0.0 all-reduce.3.cloned.1.call-start
  6.6 2.7 fusion.13
  9.3 1.2 broadcast_select_fusion
  10.6 0.3 copy.21
  10.8 0.0 copy-done.17
  10.8 0.0 copy-done.10
  10.8 0.0 copy-start.2
  10.9 0.0 copy-start.11
  10.9 4.2 %fusion.52 = bf16[8,256,192]{1,2,0:T(8,128)(2,1)} fusion(bf16[8,256,768]{2,1,0:T(8,128)(2,1)} %param.19, f32[768]{0:T(1024)S(1)} %copy-done.17, f32[8,256]{1,0:T(8,128)S(1)} %add_rsqrt_fusion.2, bf16[768,192]{0,1:T(8,128)(2,1)S(1)} %copy-done.10), kind=kOutput, calls=%fused_computation.57 | convolution fusion | flops 610664448 | bytes 4238336 | tf_op jit(solution)/shard_map/bld,dk->blk/dot_general | solution.py:17
  15.1 0.0 copy-done.2
  15.1 0.0 copy-done.11
  15.1 2.2 fusion.55
  17.3 0.0 copy-done.12
  17.3 2.2 fusion.49
  19.5 6.1 %fusion.79 = (f32[8,3,256]{2,1,0:T(4,128)S(1)}, f32[8,3,256,256]{2,3,1,0:T(8,128)}) fusion(f32[3,256,256]{1,2,0:T(8,128)S(1)} %copy.21, bf16[8,256,3,64]{1,3,2,0:T(8,128)(2,1)} %bitcast.117, bf16[8,256,3,64]{1,3,2,0:T(8,128)(2,1)} %bitcast.116), kind=kOutput, calls=%fused_computation.90 | convolution fusion | flops 206045440 | bytes 8675328 | tf_op jit(solution)/shard_map/sub | solution.py:26
  25.6 0.0 copy-done.13
  25.6 0.0 copy-start.8
  25.6 0.0 copy-start.14
  25.7 6.3 %bitcast_convert_fusion.1 = bf16[8,256,768]{2,1,0:T(8,128)(2,1)} fusion(bf16[3,64,768,1]{2,1,0,3:T(8,128)(2,1)S(1)} %bitcast.113, bf16[8,256,3,64]{1,3,2,0:T(8,128)(2,1)} %bitcast.115, f32[8,3,256,256]{2,3,1,0:T(8,128)} %get-tuple-element.10, f32[8,3,256]{2,1,0:T(4,128)S(1)} %get-tuple-element.9), kind=kOutput, calls=%fused_computation.31 | convolution fusion | flops 810418176 | bytes 10543104 | tf_op jit(solution)/shard_map/cirf,ife->cre/dot_general | solution.py:29
  32.0 0.1 all-reduce.3.cloned.1.call-update
  32.0 0.4 all-reduce.5.cloned.1.call-start
  32.4 0.0 copy-done.8
  32.4 0.0 copy-done
  32.4 0.0 copy-done.14
  32.4 1.4 convolution_convert_fusion.1
  33.8 0.0 copy-done.15
  33.8 1.4 convolution_convert_fusion
  35.3 71.1 %all-reduce.3.cloned.1.call-done = bf16[8,256,768]{2,1,0:T(8,128)(2,1)} async-done(((bf16[8,256,768]{2,1,0:T(8,128)(2,1)}), bf16[8,256,768]{2,1,0:T(8,128)(2,1)}) %all-reduce.3.cloned.1.call-update) | async-done | bytes 3145744 | tf_op jit(solution)/shard_map/psum | solution.py:81
  106.3 4.0 %fusion.17 = (f32[8,256]{1,0:T(8,128)S(1)}, bf16[8,256,768]{2,1,0:T(8,128)(2,1)S(1)}) fusion(bf16[8,256,768]{2,1,0:T(8,128)(2,1)} %all-reduce.3.cloned.1.call-done, bf16[8,256,768]{2,1,0:T(8,128)(2,1)} %param.19), kind=kLoop, calls=%fused_computation.24 | loop fusion | flops 11008000 | bytes 9445376 | tf_op jit(solution)/shard_map/reduce_sum | solution.py:12
  110.4 0.0 copy-done.16
  110.4 0.0 copy-done.18
  110.4 2.2 fusion.58
  112.6 4.0 %fusion.80 = (f32[8,3,256]{2,1,0:T(4,128)S(1)}, f32[8,3,256,128]{2,3,1,0:T(8,128)}) fusion(f32[8,128]{1,0:T(8,128)S(1)} %compare_select_fusion, bf16[8,256,3,64]{1,3,2,0:T(8,128)(2,1)} %bitcast.118, bf16[8,128,3,64]{1,3,2,0:T(8,128)(2,1)} %bitcast.120), kind=kOutput, calls=%fused_computation.91 | convolution fusion | flops 103022720 | bytes 4354048 | tf_op jit(solution)/shard_map/sub | solution.py:26
  116.6 4.9 %bitcast_convert_fusion = bf16[8,256,768]{2,1,0:T(8,128)(2,1)} fusion(bf16[3,64,768,1]{2,1,0,3:T(8,128)(2,1)} %bitcast.114, bf16[8,128,3,64]{1,3,2,0:T(8,128)(2,1)} %bitcast.119, f32[8,3,256,128]{2,3,1,0:T(8,128)} %get-tuple-element.12, f32[8,3,256]{2,1,0:T(4,128)S(1)} %get-tuple-element.11), kind=kOutput, calls=%fused_computation.30 | convolution fusion | flops 708182016 | bytes 7004160 | tf_op jit(solution)/shard_map/cirf,ife->cre/dot_general | solution.py:29
  121.5 0.1 all-reduce.5.cloned.1.call-update
  121.6 0.0 copy-done.7
  121.6 0.7 fusion.73
  122.4 16.4 %reduce-window.6 = s32[32,16,128]{2,1,0:T(8,128)S(1)} reduce-window(s32[32,16,128]{2,1,0:T(8,128)} %fusion.73, s32[]{:T(128)} %constant.13.clone.1), window={size=1x1x128 pad=0_0x0_0x127_0}, to_apply=%region_12.13 | reduce-window | flops 8323072 | bytes 524292 | tf_op jit(solution)/shard_map/reduce-window
  138.8 0.8 slice.8
  139.6 1.2 copy.30
  140.8 0.2 reduce-window.9
  141.0 0.1 add_add_fusion
  141.1 0.1 fusion.72
  141.2 50.8 %all-reduce.5.cloned.1.call-done = bf16[8,256,768]{2,1,0:T(8,128)(2,1)} async-done(((bf16[8,256,768]{2,1,0:T(8,128)(2,1)}), bf16[8,256,768]{2,1,0:T(8,128)(2,1)}) %all-reduce.5.cloned.1.call-update) | async-done | bytes 3145744 | tf_op jit(solution)/shard_map/psum | solution.py:86
  192.1 3.1 multiply_reduce_fusion
  195.2 0.0 copy-done.9
  195.2 0.0 copy-done.3
  195.2 3.3 multiply_convert_fusion
  198.5 10.5 %fusion.23 = bf16[2560,768]{1,0:T(8,128)(2,1)S(1)} fusion(bf16[2048,768]{1,0:T(8,128)(2,1)S(1)} %bitcast.102, s32[2048]{0:T(1024)S(1)} %add_select_fusion), kind=kOutput, calls=%fused_computation.38 | convolution fusion | flops 8060272640 | bytes 7086080 | tf_op jit(solution)/shard_map/sc,sd->cd/dot_general | solution.py:52
  209.0 0.0 copy-done.4
  209.0 51.0 %all_to_all.10 = bf16[32,80,768]{2,1,0:T(8,128)(2,1)} all-to-all(bf16[32,80,768]{2,1,0:T(8,128)(2,1)S(1)} %bitcast.105), channel_id=1, replica_groups=mesh['part'=1,'tp'=4,'ep'=8] {'ep'}, dimensions={0} | all-to-all | bytes 7864320 | tf_op jit(solution)/shard_map/all_to_all | solution.py:53
  260.0 22.6 %fusion.6 = bf16[4,8,80,3072]{3,2,1,0:T(8,128)(2,1)} fusion(bf16[4,768,3072]{2,1,0:T(8,128)(2,1)} %param.36, bf16[8,4,80,768]{3,2,1,0:T(8,128)(2,1)} %bitcast.104), kind=kOutput, calls=%fused_computation.8 | convolution fusion | flops 12079595520 | bytes 38535168 | tf_op jit(solution)/shard_map/gecd,edf->gecf/dot_general | solution.py:55
  282.6 22.4 %convert_bitcast_fusion = bf16[8,4,80,768]{3,2,0,1:T(8,128)(2,1)} fusion(bf16[4,3072,768]{2,1,0:T(8,128)(2,1)} %param.37, bf16[4,8,80,3072]{3,2,1,0:T(8,128)(2,1)} %fusion.6), kind=kOutput, calls=%fused_computation.40 | convolution fusion | flops 12105154560 | bytes 38535168 | tf_op jit(solution)/shard_map/gecf,efd->gecd/dot_general | solution.py:56
  305.1 4.3 %copy.24 = bf16[8,4,80,768]{3,2,1,0:T(8,128)(2,1)} copy(bf16[8,4,80,768]{3,2,0,1:T(8,128)(2,1)} %convert_bitcast_fusion) | data formatting | bytes 7864320 | tf_op jit(solution)/shard_map/convert_element_type | solution.py:56
  309.4 6.2 %all-to-all-start.1 = ((bf16[32,80,768]{2,1,0:T(8,128)(2,1)}), bf16[32,80,768]{2,1,0:T(8,128)(2,1)}, u32[]{:S(2)}, u32[]{:S(2)}) async-start(bf16[32,80,768]{2,1,0:T(8,128)(2,1)} %bitcast.101), calls=%async_computation.1 | async-start | bytes 7864320 | tf_op jit(solution)/shard_map/all_to_all | solution.py:57
  315.6 0.0 copy-done.5
  315.6 0.0 copy-done.6
  315.6 2.8 fusion.81
  318.4 0.1 fusion.76
  318.5 0.1 multiply_reduce_fusion.1
  318.6 42.7 %all-to-all-done.1 = bf16[32,80,768]{2,1,0:T(8,128)(2,1)} async-done(((bf16[32,80,768]{2,1,0:T(8,128)(2,1)}), bf16[32,80,768]{2,1,0:T(8,128)(2,1)}, u32[]{:S(2)}, u32[]{:S(2)}) %all-to-all-start.1) | async-done | bytes 3932192 | tf_op jit(solution)/shard_map/all_to_all | solution.py:57
  361.3 13.7 %fusion.21 = bf16[2048,768]{1,0:T(8,128)(2,1)} fusion(f32[8,256,768]{2,1,0:T(8,128)} %get-tuple-element.8, bf16[2560,768]{1,0:T(8,128)(2,1)} %bitcast.34, s32[2048]{0:T(1024)S(1)} %add_select_fusion, f32[2048]{0:T(1024)S(1)} %multiply_reduce_fusion.1), kind=kOutput, calls=%fused_computation.29 | convolution fusion | flops 8063025152 | bytes 13385728 | tf_op jit(solution)/shard_map/sc,cd->sd/dot_general | solution.py:58
  375.0 0.0 copy-done.1
  (22 shorter events, 0.1 us)
Async XLA Ops:
  6.5 25.9 %copy-start = (bf16[8,128,768]{2,1,0:T(8,128)(2,1)S(1)}, bf16[8,128,768]{2,1,0:T(8,128)(2,1)}, u32[]{:S(2)}) copy-start(bf16[8,128,768]{2,1,0:T(8,128)(2,1)} %param.20) | copy-start | bytes 4718596
  6.6 4.3 %copy-start.17 = (f32[768]{0:T(1024)S(1)}, f32[768]{0:T(1024)}, u32[]{:S(2)}) copy-start(f32[768]{0:T(1024)} %param.24) | copy-start | bytes 9220
  6.6 4.3 %copy-start.10 = (bf16[768,192]{0,1:T(8,128)(2,1)S(1)}, bf16[768,192]{0,1:T(8,128)(2,1)}, u32[]{:S(2)}) copy-start(bf16[768,192]{0,1:T(8,128)(2,1)} %param.26) | copy-start | bytes 884740
  6.6 99.8 %all-reduce.3.cloned.1.call-start = ((), (), s32[]{:S(2)}) async-start(), calls=%async_computation.2 | async-start | bytes 6291456 | tf_op jit(solution)/shard_map/psum | solution.py:81
  10.8 4.2 %copy-start.2 = (bf16[8,256,768]{2,1,0:T(8,128)(2,1)S(1)}, bf16[8,256,768]{2,1,0:T(8,128)(2,1)}, u32[]{:S(2)}) copy-start(bf16[8,256,768]{2,1,0:T(8,128)(2,1)} %param.19) | copy-start | bytes 9437188
  10.9 4.2 %copy-start.11 = (bf16[768,192]{0,1:T(8,128)(2,1)S(1)}, bf16[768,192]{0,1:T(8,128)(2,1)}, u32[]{:S(2)}) copy-start(bf16[768,192]{0,1:T(8,128)(2,1)} %param.27) | copy-start | bytes 884740
  15.1 2.2 copy-start.12
  19.5 6.1 %copy-start.13 = (bf16[192,768]{1,0:T(8,128)(2,1)S(1)}, bf16[192,768]{1,0:T(8,128)(2,1)}, u32[]{:S(2)}) copy-start(bf16[192,768]{1,0:T(8,128)(2,1)} %param.28) | copy-start | bytes 884740
  25.6 6.8 %copy-start.8 = (s32[8,128]{1,0:T(8,128)S(1)}, s32[8,128]{1,0:T(8,128)}, u32[]{:S(2)}) copy-start(s32[8,128]{1,0:T(8,128)} %param.21) | copy-start | bytes 12292
  25.6 6.8 %copy-start.14 = (bf16[768,192]{0,1:T(8,128)(2,1)S(1)}, bf16[768,192]{0,1:T(8,128)(2,1)}, u32[]{:S(2)}) copy-start(bf16[768,192]{0,1:T(8,128)(2,1)} %param.31) | copy-start | bytes 884740
  32.0 1.9 copy-start.15
  32.0 160.0 %all-reduce.5.cloned.1.call-start = ((), (), s32[]{:S(2)}) async-start(), calls=%async_computation.3 | async-start | bytes 6291456 | tf_op jit(solution)/shard_map/psum | solution.py:86
  35.2 75.1 %copy-start.16 = (bf16[768,192]{0,1:T(8,128)(2,1)S(1)}, bf16[768,192]{0,1:T(8,128)(2,1)}, u32[]{:S(2)}) copy-start(bf16[768,192]{0,1:T(8,128)(2,1)} %param.30) | copy-start | bytes 884740
  35.2 75.2 %copy-start.18 = (f32[768]{0:T(1024)S(1)}, f32[768]{0:T(1024)}, u32[]{:S(2)}) copy-start(f32[768]{0:T(1024)} %param.29) | copy-start | bytes 9220
  116.6 5.0 %copy-start.7 = (s32[8,256]{1,0:T(8,128)S(1)}, s32[8,256]{1,0:T(8,128)}, u32[]{:S(2)}) copy-start(s32[8,256]{1,0:T(8,128)} %param.22) | copy-start | bytes 24580
  121.5 73.7 %copy-start.9 = (f32[768]{0:T(1024)S(1)}, f32[768]{0:T(1024)}, u32[]{:S(2)}) copy-start(f32[768]{0:T(1024)} %param.34) | copy-start | bytes 9220
  192.0 3.2 copy-start.3
  198.5 10.5 %copy-start.4 = (bf16[8,256,768]{2,1,0:T(8,128)(2,1)}, bf16[8,256,768]{2,1,0:T(8,128)(2,1)S(1)}, u32[]{:S(2)}) copy-start(bf16[8,256,768]{2,1,0:T(8,128)(2,1)S(1)} %get-tuple-element.7) | copy-start | bytes 9437188
  309.4 6.2 %copy-start.5 = (bf16[8,256,768]{2,1,0:T(8,128)(2,1)S(1)}, bf16[8,256,768]{2,1,0:T(8,128)(2,1)}, u32[]{:S(2)}) copy-start(bf16[8,256,768]{2,1,0:T(8,128)(2,1)} %copy-done.4) | copy-start | bytes 9437188
  309.4 6.2 %copy-start.6 = (f32[768,32]{0,1:T(8,128)S(1)}, f32[768,32]{0,1:T(8,128)}, u32[]{:S(2)}) copy-start(f32[768,32]{0,1:T(8,128)} %param.35) | copy-start | bytes 294916
  309.4 51.9 %all-to-all-start.1 = ((bf16[32,80,768]{2,1,0:T(8,128)(2,1)}), bf16[32,80,768]{2,1,0:T(8,128)(2,1)}, u32[]{:S(2)}, u32[]{:S(2)}) async-start(bf16[32,80,768]{2,1,0:T(8,128)(2,1)} %bitcast.101), calls=%async_computation.1 | async-start | bytes 7864320 | tf_op jit(solution)/shard_map/all_to_all | solution.py:57
  361.3 13.7 %copy-start.1 = (bf16[8,128,768]{2,1,0:T(8,128)(2,1)S(1)}, bf16[8,128,768]{2,1,0:T(8,128)(2,1)}, u32[]{:S(2)}) copy-start(bf16[8,128,768]{2,1,0:T(8,128)(2,1)} %param.20) | copy-start | bytes 4718596
Sparse Core Ops, SparseCore 0:
  32.1 74.1 all-reduce.2
  121.7 70.2 all-reduce.4
where the time goes:
time: 389 us; the launch traced here: 382 us
  waiting for transfers between devices  165 us (42%)
  matrix products  107 us (28%)
  blocking collectives  51 us (13%)
  other arithmetic  32.1 us (8%)
  between operations  13.9 us (4%)
  local copies, waits for them, and re-layouts  6.72 us (2%)
  starting transfers between devices  6.52 us (2%)
    psum x2, waiting for transfers between devices, layer(): attn_sum = lax.psum(partial.astype(jnp.bfloat16), 'tp')  122 us
    all_to_all x1, blocking collectives, expert_layer(): lax.all_to_all(send_buf.reshape(experts, capacity, d_model), 'ep', 0, 0,...  51 us
    all_to_all x1, waiting for transfers between devices, expert_layer(): lax.all_to_all(expert_out.reshape(experts, capacity, d_model), 'ep', 0, 0...  42.7 us
    dot_general x1, matrix products, expert_layer(): jnp.einsum('gecd,edf->gecf', received, w_in, preferred_element_type=jnp.f...  22.6 us
    dot_general x1, matrix products, expert_layer(): jnp.einsum('gecf,efd->gecd', hidden, w_out, preferred_element_type=jnp.fl...  22.4 us
    another operation x2, other arithmetic  16.6 us
    dot_general x1, matrix products, expert_layer(): jnp.einsum('sc,cd->sd', dispatch, returned.reshape(experts * capacity, d_...  13.7 us
    dot_general x6, matrix products, head_project(): jnp.einsum('bld,dk->blk', states, weight, preferred_element_type=jnp.floa...  13.6 us
  transfers between devices with their start and end apart: 3, of which 3 were waited for; matrix products, arithmetic and copies ran while one was open for 7% of the time, Pallas kernels for 0%

commit v1 on v0

v1 whole, which is shorter than its diff:
```python
import jax
import jax.numpy as jnp
from jax import lax
from jax.sharding import PartitionSpec as P

EPSILON = 1e-6
NEG_LARGE = -1e30


def rms_norm(states, gain_vec):
    upcast = states.astype(jnp.float32)
    mean_sq = jnp.mean(upcast * upcast, axis=-1, keepdims=True)
    return (upcast * lax.rsqrt(mean_sq + EPSILON) * gain_vec).astype(jnp.bfloat16)


def matmul_f32(left, right):
    return jnp.dot(left, right, preferred_element_type=jnp.float32)


def split_heads(flat, heads):
    return flat.reshape(flat.shape[0], flat.shape[1], heads, flat.shape[2] // heads)


def attention_context(queries, key_heads, values, bias_mask):
    scores = jnp.einsum('bqhe,bkhe->bhqk', queries, key_heads, preferred_element_type=jnp.float32) + bias_mask
    weights = jax.nn.softmax(scores, axis=-1).astype(jnp.bfloat16)
    context = jnp.einsum('bhqk,bkhe->bqhe', weights, values, preferred_element_type=jnp.float32).astype(jnp.bfloat16)
    return context.reshape(context.shape[0], context.shape[1], -1)


def split_three(weight):
    high = weight.astype(jnp.bfloat16)
    rest = weight - high.astype(jnp.float32)
    mid = rest.astype(jnp.bfloat16)
    low = (rest - mid.astype(jnp.float32)).astype(jnp.bfloat16)
    return high, mid, low


def token_positions(choice, experts):
    tokens = choice.shape[0]
    block = 128
    one_hot = (choice[:, None] == lax.broadcasted_iota(jnp.int32, (tokens, experts), 1)).astype(jnp.bfloat16)
    blocks = one_hot.reshape(tokens // block, block, experts)
    lower = (lax.broadcasted_iota(jnp.int32, (block, block), 0) >= lax.broadcasted_iota(jnp.int32, (block, block), 1)).astype(jnp.bfloat16)
    inside = jnp.einsum('ij,bje->bie', lower, blocks, preferred_element_type=jnp.float32)
    totals = inside[:, -1, :]
    before = jnp.cumsum(totals, axis=0) - totals
    counts = (inside + before[:, None, :]).reshape(tokens, experts)
    return (jnp.sum(counts * one_hot.astype(jnp.float32), axis=-1) - 1.0).astype(jnp.int32)


def solution(mesh):
    ep_size = mesh.shape['ep']
    tp_size = mesh.shape['tp']
    token_spec = P(('part', 'ep'), None, None)
    row_spec = P(('part', 'ep'), None)
    col_spec = P(None, 'tp')
    head_rows = P('tp', None)
    vec_spec = P(None)
    expert_spec = P('ep', None, None)
    in_specs = (token_spec, token_spec, row_spec, row_spec, P('tp', None, None), vec_spec, col_spec, col_spec, col_spec, head_rows, vec_spec, col_spec, col_spec, col_spec, head_rows, vec_spec, P(None, None), expert_spec, expert_spec)

    def layer(dec_states, enc_states, enc_pad, expert_idx, self_bias, gain_self, wq_self, wk_self, wv_self, wo_self, gain_cross, wq_cross, wk_cross, wv_cross, wo_cross, gain_ffn, w_router, w_in, w_out):
        batch_dev, dec_len, d_model = dec_states.shape
        heads = self_bias.shape[0]
        width = wo_self.shape[0]
        own_batch = batch_dev // tp_size
        tp_id = lax.axis_index('tp')

        w_pack = jnp.concatenate([wo_self, wo_cross, wq_cross.T], axis=0)
        w_all = lax.all_gather(w_pack, 'tp', axis=0, tiled=False)
        wo_self_all = w_all[:, :width].reshape(tp_size * width, d_model)
        wo_cross_all = w_all[:, width:2 * width].reshape(tp_size * width, d_model)
        wq_cross_all = w_all[:, 2 * width:].reshape(tp_size * width, d_model)

        kv_local = jnp.concatenate([matmul_f32(enc_states, wk_cross), matmul_f32(enc_states, wv_cross)], axis=-1).astype(jnp.bfloat16)
        kv_own = lax.all_to_all(kv_local.reshape(tp_size, own_batch, -1, 2 * width), 'tp', 0, 0, tiled=True)

        row_ids = lax.broadcasted_iota(jnp.int32, (dec_len, dec_len), 0)
        col_ids = lax.broadcasted_iota(jnp.int32, (dec_len, dec_len), 1)
        causal_bias = jnp.where(col_ids <= row_ids, self_bias, NEG_LARGE)[None]
        normed = rms_norm(dec_states, gain_self)
        queries = split_heads(matmul_f32(normed, wq_self).astype(jnp.bfloat16), heads)
        key_heads = split_heads(matmul_f32(normed, wk_self).astype(jnp.bfloat16), heads)
        values = split_heads(matmul_f32(normed, wv_self).astype(jnp.bfloat16), heads)
        context = attention_context(queries, key_heads, values, causal_bias)
        context = lax.all_to_all(context, 'tp', 0, 2, tiled=True)
        dec_own = lax.dynamic_slice_in_dim(dec_states, tp_id * own_batch, own_batch, 0)
        after_self = (dec_own.astype(jnp.float32) + matmul_f32(context, wo_self_all)).astype(jnp.bfloat16)

        pad_own = lax.dynamic_slice_in_dim(enc_pad, tp_id * own_batch, own_batch, 0)
        pad_bias = jnp.where(pad_own == 0, 0.0, NEG_LARGE).astype(jnp.float32)[:, None, None, :]
        normed = rms_norm(after_self, gain_cross)
        all_heads = heads * tp_size
        queries = jnp.einsum('bld,kd->blk', normed, wq_cross_all, preferred_element_type=jnp.float32).astype(jnp.bfloat16)
        kv_own = jnp.transpose(kv_own, (1, 2, 0, 3))
        k_own = kv_own[..., :width].reshape(own_batch, -1, tp_size * width)
        v_own = kv_own[..., width:].reshape(own_batch, -1, tp_size * width)
        context = attention_context(split_heads(queries, all_heads), split_heads(k_own, all_heads), split_heads(v_own, all_heads), pad_bias)
        after_cross = (after_self.astype(jnp.float32) + matmul_f32(context, wo_cross_all)).astype(jnp.bfloat16)
        after_cross = lax.all_gather(after_cross, 'tp', axis=0, tiled=True)

        tokens = batch_dev * dec_len
        experts = w_router.shape[1]
        capacity = (5 * tokens + 4 * experts - 1) // (4 * experts)
        row_cap = -(-capacity // tp_size)
        slots = experts * row_cap
        choice = expert_idx.reshape(tokens)
        position = token_positions(choice, experts)
        kept = position < capacity
        slot_row = position // row_cap
        local_slot = choice * row_cap + position % row_cap
        slot_here = jnp.where(kept & (slot_row == tp_id), local_slot, -1)
        slot_full = jnp.where(kept, slot_row * slots + local_slot, -1)

        states = after_cross.reshape(tokens, d_model)
        normed = rms_norm(states, gain_ffn)
        dispatch = (lax.broadcasted_iota(jnp.int32, (slots, tokens), 0) == slot_here[None, :]).astype(jnp.bfloat16)
        send_buf = matmul_f32(dispatch, normed).astype(jnp.bfloat16)
        local_experts = experts // ep_size
        received = lax.all_to_all(send_buf.reshape(ep_size, local_experts * row_cap, d_model), 'ep', 0, 0, tiled=True)
        received = received.reshape(ep_size, local_experts, row_cap, d_model)
        received = jnp.transpose(received, (1, 0, 2, 3)).reshape(local_experts, ep_size * row_cap, d_model)
        hidden = jnp.maximum(jnp.einsum('ecd,edf->ecf', received, w_in, preferred_element_type=jnp.float32), 0.0).astype(jnp.bfloat16)
        expert_out = jnp.einsum('ecf,efd->ecd', hidden, w_out, preferred_element_type=jnp.float32).astype(jnp.bfloat16)
        expert_out = jnp.transpose(expert_out.reshape(local_experts, ep_size, row_cap, d_model), (1, 0, 2, 3))
        returned = lax.all_to_all(expert_out.reshape(ep_size, local_experts * row_cap, d_model), 'ep', 0, 0, tiled=True)
        all_slots = lax.all_gather(returned.reshape(slots, d_model), 'tp', axis=0, tiled=True)

        logits = sum(matmul_f32(normed, piece) for piece in split_three(w_router))
        router_prob = jax.nn.softmax(logits, axis=-1)
        gate_prob = jnp.sum(jnp.where(choice[:, None] == lax.broadcasted_iota(jnp.int32, (tokens, experts), 1), router_prob, 0.0), axis=-1)
        pick = (slot_full[:, None] == lax.broadcasted_iota(jnp.int32, (tokens, tp_size * slots), 1)).astype(jnp.bfloat16)
        combined = matmul_f32(pick, all_slots)
        result = states.astype(jnp.float32) + gate_prob[:, None] * combined
        return result.astype(jnp.bfloat16).reshape(batch_dev, dec_len, d_model)

    return jax.shard_map(layer, mesh=mesh, in_specs=in_specs, out_specs=token_spec, check_vma=False)
```

time: 389 us -> 246 us (0.63); the launches traced: 382 us -> 246 us
  waiting for transfers between devices: 165 us -> 93.7 us
  matrix products: 107 us -> 65.1 us
  other arithmetic: 32.1 us -> 10.9 us
  blocking collectives: 51 us -> 37.6 us
  local copies, waits for them, and re-layouts: 6.72 us -> 13.6 us
  starting transfers between devices: 6.52 us -> 11.2 us
    psum x2 -> x0, waiting for transfers between devices: 122 us -> none  [layer(): attn_sum = lax.psum(partial.astype(jnp.bfloat16), 'tp')]
    all_gather x0 -> x3, waiting for transfers between devices: none -> 93.5 us  [the longest x1 38.7 us: layer(): lax.all_gather(returned.reshape(slots, d_model), 'tp', axis=0, tiled=True)]
    all_to_all x1 -> x2, waiting for transfers between devices: 42.7 us -> 0.01 us  [the longest x1 0.01 us: layer(): lax.all_to_all(kv_local.reshape(tp_size, own_batch, -1, 2 * width), 'tp',...]
    dot_general x13 -> x17, matrix products: 96.9 us -> 56.1 us  [the longest x12 31.8 us: matmul_f32(): return jnp.dot(left, right, preferred_element_type=jnp.float32)]
    another operation x2 -> x1, other arithmetic: 16.6 us -> 0.02 us  [token_positions(): before = jnp.cumsum(totals, axis=0) - totals]
    all_to_all x1 -> x2, blocking collectives: 51 us -> 37.6 us  [the longest x1 19.3 us: layer(): lax.all_to_all(send_buf.reshape(ep_size, local_experts * row_cap, d_model...]
    reduce_sum x3 -> x2, other arithmetic: 9.86 us -> 3.4 us  [rms_norm(): mean_sq = jnp.mean(upcast * upcast, axis=-1, keepdims=True)]
    all_to_all x1 -> x2, starting transfers between devices: 6.16 us -> 10.9 us  [the longest x1 6.6 us: layer(): lax.all_to_all(kv_local.reshape(tp_size, own_batch, -1, 2 * width), 'tp',...]
  transfers between devices with their start and end apart: 3 -> 5, of which waited for: 3 -> 3; matrix products, arithmetic and copies ran while one was open for 7% -> 15% of each run, Pallas kernels for 0% -> 0%
where the time goes in v1:
time: 246 us
  waiting for transfers between devices  93.7 us (38%)
  matrix products  65.1 us (26%)
  blocking collectives  37.6 us (15%)
  local copies, waits for them, and re-layouts  13.6 us (6%)
  between operations  13.5 us (5%)
  starting transfers between devices  11.2 us (5%)
  other arithmetic  10.9 us (4%)
    all_gather x1, waiting for transfers between devices, layer(): lax.all_gather(returned.reshape(slots, d_model), 'tp', axis=0, tiled=True)  38.7 us
    all_gather x1, waiting for transfers between devices, layer(): after_cross = lax.all_gather(after_cross, 'tp', axis=0, tiled=True)  35.2 us
    dot_general x12, matrix products, matmul_f32(): return jnp.dot(left, right, preferred_element_type=jnp.float32)  31.8 us
    all_gather x1, waiting for transfers between devices, layer(): w_all = lax.all_gather(w_pack, 'tp', axis=0, tiled=False)  19.6 us
    all_to_all x1, blocking collectives, layer(): lax.all_to_all(send_buf.reshape(ep_size, local_experts * row_cap, d_model...  19.3 us
    all_to_all x1, blocking collectives, layer(): lax.all_to_all(expert_out.reshape(ep_size, local_experts * row_cap, d_mod...  18.3 us
    dot_general x1, matrix products, layer(): jnp.einsum('ecf,efd->ecd', hidden, w_out, preferred_element_type=jnp.floa...  16.3 us
    sub x2, matrix products, attention_context(): weights = jax.nn.softmax(scores, axis=-1).astype(jnp.bfloat16)  9.06 us
  transfers between devices with their start and end apart: 5, of which 3 were waited for; matrix products, arithmetic and copies ran while one was open for 15% of the time, Pallas kernels for 0%

profile of v1, /device:TPU:97, one launch (start us, length us, event | category | flops | bytes accessed | tf_op | source)
XLA Modules:
  0.0 245.6 jit_solution(4441406306837261963)
XLA Ops:
  6.6 2.2 pad_maximum_fusion
  8.8 0.1 all-gather.9.cloned.1.call-update
  8.9 1.6 convolution_convert_fusion.2
  10.5 0.7 convolution_convert_fusion.1
  11.2 0.0 copy-start.3
  11.2 0.9 pad_maximum_fusion.1
  12.1 6.6 %all-to-all-start.1 = ((bf16[4,2,128,384]{2,3,1,0:T(8,128)(2,1)}), bf16[4,2,128,384]{2,3,1,0:T(8,128)(2,1)}, u32[]{:S(2)}, u32[]{:S(2)}) async-start(bf16[4,2,128,384]{2,3,1,0:T(8,128)(2,1)} %pad_maximum_fusion.1), calls=%async_computation.1 | async-start | bytes 1572864 | tf_op jit(solution)/shard_map/all_to_all | solution.py:77
  18.8 0.0 copy-start.11
  18.8 0.0 copy-start.14
  18.8 2.1 broadcast_select_fusion
  20.9 2.3 copy.58
  23.2 0.7 fusion.4
  23.9 0.0 copy-start.12
  23.9 2.2 fusion.40
  26.1 2.2 fusion.43
  28.3 2.2 fusion.37
  30.5 6.3 %fusion.80 = (f32[8,3,256]{2,1,0:T(4,128)S(1)}, f32[8,3,256,256]{2,3,1,0:T(8,128)}) fusion(f32[3,256,256]{1,2,0:T(8,128)} %copy.58, bf16[8,256,3,64]{1,3,2,0:T(8,128)(2,1)} %bitcast.168, bf16[8,256,3,64]{1,3,2,0:T(8,128)(2,1)} %bitcast.169), kind=kOutput, calls=%fused_computation.111 | convolution fusion | flops 206045440 | bytes 8675328 | tf_op jit(solution)/shard_map/sub | solution.py:26
  36.8 4.6 %fusion.47 = bf16[8,3,64,256]{3,2,1,0:T(8,128)(2,1)} fusion(bf16[8,256,3,64]{1,3,2,0:T(8,128)(2,1)} %bitcast.167, f32[8,3,256,256]{2,3,1,0:T(8,128)} %get-tuple-element.12, f32[8,3,256]{2,1,0:T(4,128)S(1)} %get-tuple-element.11), kind=kOutput, calls=%fused_computation.55 | convolution fusion | flops 204865536 | bytes 7888896 | tf_op jit(solution)/shard_map/bhqk,bkhe->bqhe/dot_general | solution.py:27
  41.4 0.0 all-to-all-done.1
  41.4 4.3 %all-to-all-start = ((bf16[8,256,192]{1,2,0:T(8,128)(2,1)}), bf16[8,256,192]{1,2,0:T(8,128)(2,1)}, u32[]{:S(2)}, u32[]{:S(2)}) async-start(bf16[8,256,192]{1,2,0:T(8,128)(2,1)} %bitcast.155), calls=%async_computation | async-start | bytes 1572864 | tf_op jit(solution)/shard_map/all_to_all | solution.py:87
  45.7 0.2 all-gather.5.cloned.1.call-start
  45.9 0.7 compare_select_fusion
  46.6 1.2 fusion.79
  47.8 0.8 copy.62
  48.6 19.6 %all-gather.9.cloned.1.call-done = bf16[2304,768]{1,0:T(8,128)(2,1)} async-done(((bf16[576,768]{1,0:T(8,128)(2,1)}), bf16[2304,768]{1,0:T(8,128)(2,1)}) %all-gather.9.cloned.1.call-update) | async-done | bytes 3538960 | tf_op jit(solution)/shard_map/all_gather | solution.py:71
  68.3 3.2 %fusion.78 = (bf16[4,192,768]{2,1,0:T(8,128)(2,1)}, bf16[4,192,768]{2,1,0:T(8,128)(2,1)}) fusion(bf16[4,576,768]{2,1,0:T(8,128)(2,1)} %bitcast.149), kind=kLoop, calls=%fused_computation.109 | loop fusion | bytes 4718592 | tf_op jit(solution)/shard_map/slice | solution.py:73
  71.5 2.5 %fusion.28 = (f32[2,256]{1,0:T(2,128)S(1)}, bf16[2,256,768]{2,1,0:T(8,128)(2,1)S(1)}) fusion(bf16[2,256,4,192]{1,3,0,2:T(8,128)(2,1)} %bitcast.9, bf16[4,576,768]{2,1,0:T(8,128)(2,1)} %bitcast.150, bf16[8,256,768]{2,1,0:T(8,128)(2,1)S(1)} %copy-done.3, s32[]{:T(128)S(6)} %select_n.59), kind=kOutput, calls=%fused_computation.40 | convolution fusion | flops 606338560 | bytes 3540996 | tf_op jit(solution)/shard_map/dot_general | solution.py:17
  74.0 0.9 copy-done.16
  74.9 0.8 convolution_convert_fusion
  75.8 0.3 copy.61
  76.1 2.8 %fusion.81 = (f32[2,12,256]{2,1,0:T(8,128)S(1)}, f32[2,12,256,128]{2,3,1,0:T(8,128)}) fusion(f32[2,128]{1,0:T(2,128)S(1)} %compare_select_fusion, bf16[2,256,12,64]{1,3,2,0:T(8,128)(2,1)S(1)} %bitcast.156, bf16[2,128,12,64]{1,3,2,0:T(8,128)(2,1)S(1)} %bitcast.158), kind=kOutput, calls=%fused_computation.112 | convolution fusion | flops 103022720 | bytes 4350976 | tf_op jit(solution)/shard_map/sub | solution.py:26
  78.8 2.4 fusion.46
  81.2 0.0 copy-start.8
  81.3 1.7 fusion.31
  83.0 0.1 all-gather.5.cloned.1.call-update
  83.1 0.1 all-gather.7.cloned.1.call-start
  83.2 0.2 convolution_bitcast_fusion
  83.4 0.1 slice.29
  83.5 0.2 copy.65
  83.7 0.2 copy.66
  83.9 0.3 subtract_reduce_fusion
  84.1 0.1 multiply_reduce_fusion
  84.3 35.2 %all-gather.5.cloned.1.call-done = bf16[8,256,768]{2,1,0:T(8,128)(2,1)} async-done(((bf16[2,256,768]{2,1,0:T(8,128)(2,1)}), bf16[8,256,768]{2,1,0:T(8,128)(2,1)}) %all-gather.5.cloned.1.call-update) | async-done | bytes 3145744 | tf_op jit(solution)/shard_map/all_gather | solution.py:101
  119.6 2.7 %fusion.7 = f32[8,256]{1,0:T(8,128)S(1)} fusion(bf16[8,256,768]{2,1,0:T(8,128)(2,1)} %all-gather.5.cloned.1.call-done), kind=kLoop, calls=%fused_computation.14 | loop fusion | flops 4716544 | bytes 3153920 | tf_op jit(solution)/shard_map/reduce_sum | solution.py:12
  122.3 0.1 copy-done.2
  122.4 0.8 fusion.9
  123.2 2.4 fusion.36
  125.6 19.3 %all_to_all.30 = bf16[8,80,768]{2,1,0:T(8,128)(2,1)S(1)} all-to-all(bf16[8,80,768]{2,1,0:T(8,128)(2,1)S(1)} %bitcast.153), channel_id=1, replica_groups=mesh['part'=1,'tp'=4,'ep'=8] {'ep'}, dimensions={0} | all-to-all | bytes 1966080 | tf_op jit(solution)/shard_map/all_to_all | solution.py:121
  144.8 0.3 copy.67
  145.1 1.7 copy.68
  146.8 16.3 %fusion.35 = bf16[4,160,768]{2,1,0:T(8,128)(2,1)} fusion(bf16[4,3072,768]{2,1,0:T(8,128)(2,1)} %param.37, bf16[4,768,3072]{2,1,0:T(8,128)(2,1)} %param.36, bf16[4,160,768]{2,0,1:T(4,128)(2,1)} %bitcast.154), kind=kOutput, calls=%fused_computation.48 | convolution fusion | flops 6044221440 | bytes 39714816 | tf_op jit(solution)/shard_map/ecf,efd->ecd/dot_general | solution.py:125
  163.1 2.0 copy.70
  165.1 0.0 copy-start.6
  165.1 0.3 copy.71
  165.4 0.2 copy.72
  165.6 18.3 %all_to_all.31 = bf16[8,80,768]{2,1,0:T(8,128)(2,1)} all-to-all(bf16[8,80,768]{2,1,0:T(8,128)(2,1)S(1)} %copy.72), channel_id=1, replica_groups=mesh['part'=1,'tp'=4,'ep'=8] {'ep'}, dimensions={0} | all-to-all | bytes 1966080 | tf_op jit(solution)/shard_map/all_to_all | solution.py:127
  183.9 0.1 all-gather.7.cloned.1.call-update
  184.0 1.0 fusion.66
  185.0 1.0 convolution_add_fusion.1
  186.0 1.1 fusion.82
  187.1 0.1 fusion.63
  187.1 0.1 select_reduce_fusion
  187.2 38.7 %all-gather.7.cloned.1.call-done = bf16[2560,768]{1,0:T(8,128)(2,1)} async-done(((bf16[640,768]{1,0:T(8,128)(2,1)}), bf16[2560,768]{1,0:T(8,128)(2,1)}) %all-gather.7.cloned.1.call-update) | async-done | bytes 3932176 | tf_op jit(solution)/shard_map/all_gather | solution.py:128
  225.9 13.2 %fusion.10 = bf16[2048,768]{1,0:T(8,128)(2,1)} fusion(bf16[8,256,768]{2,1,0:T(8,128)(2,1)} %all-gather.5.cloned.1.call-done, bf16[2560,768]{1,0:T(8,128)(2,1)} %all-gather.7.cloned.1.call-done, s32[2048]{0:T(1024)S(1)} %get-tuple-element.5, f32[2048]{0:T(1024)S(1)} %select_reduce_fusion), kind=kOutput, calls=%fused_computation.17 | convolution fusion | flops 8064598016 | bytes 10240000 | tf_op jit(solution)/shard_map/dot_general | solution.py:17
  (41 shorter events, 0.2 us)
Async XLA Ops:
  6.5 2.3 copy-start
  6.6 4.0 %copy-start.10 = (bf16[768,192]{0,1:T(8,128)(2,1)S(1)}, bf16[768,192]{0,1:T(8,128)(2,1)}, u32[]{:S(2)}) copy-start(bf16[768,192]{0,1:T(8,128)(2,1)} %param.32) | copy-start | bytes 884740
  6.6 61.7 %all-gather.9.cloned.1.call-start = ((), (), s32[]{:S(2)}) async-start(), calls=%async_computation.6 | async-start | bytes 4423680 | tf_op jit(solution)/shard_map/all_gather | solution.py:71
  11.2 12.0 %copy-start.3 = (bf16[8,256,768]{2,1,0:T(8,128)(2,1)S(1)}, bf16[8,256,768]{2,1,0:T(8,128)(2,1)}, u32[]{:S(2)}) copy-start(bf16[8,256,768]{2,1,0:T(8,128)(2,1)} %param.19) | copy-start | bytes 9437188
  12.1 29.2 %all-to-all-start.1 = ((bf16[4,2,128,384]{2,3,1,0:T(8,128)(2,1)}), bf16[4,2,128,384]{2,3,1,0:T(8,128)(2,1)}, u32[]{:S(2)}, u32[]{:S(2)}) async-start(bf16[4,2,128,384]{2,3,1,0:T(8,128)(2,1)} %pad_maximum_fusion.1), calls=%async_computation.1 | async-start | bytes 1572864 | tf_op jit(solution)/shard_map/all_to_all | solution.py:77
  18.8 5.1 %copy-start.11 = (bf16[768,192]{0,1:T(8,128)(2,1)S(1)}, bf16[768,192]{0,1:T(8,128)(2,1)}, u32[]{:S(2)}) copy-start(bf16[768,192]{0,1:T(8,128)(2,1)} %param.25) | copy-start | bytes 884740
  18.8 5.1 %copy-start.14 = (f32[768]{0:T(1024)S(1)}, f32[768]{0:T(1024)}, u32[]{:S(2)}) copy-start(f32[768]{0:T(1024)} %param.24) | copy-start | bytes 9220
  23.9 2.2 copy-start.12
  26.1 2.2 copy-start.13
  41.4 30.1 %all-to-all-start = ((bf16[8,256,192]{1,2,0:T(8,128)(2,1)}), bf16[8,256,192]{1,2,0:T(8,128)(2,1)}, u32[]{:S(2)}, u32[]{:S(2)}) async-start(bf16[8,256,192]{1,2,0:T(8,128)(2,1)} %bitcast.155), calls=%async_computation | async-start | bytes 1572864 | tf_op jit(solution)/shard_map/all_to_all | solution.py:87
  45.7 73.9 %all-gather.5.cloned.1.call-start = ((), (), s32[]{:S(2)}) async-start(), calls=%async_computation.4 | async-start | bytes 3932160 | tf_op jit(solution)/shard_map/all_gather | solution.py:101
  71.4 3.5 %copy-start.5 = (bf16[4,192,768]{2,1,0:T(8,128)(2,1)S(1)}, bf16[4,192,768]{2,1,0:T(8,128)(2,1)}, u32[]{:S(2)}) copy-start(bf16[4,192,768]{2,1,0:T(8,128)(2,1)} %get-tuple-element.8) | copy-start | bytes 3538948
  71.5 3.5 %copy-start.15 = (f32[768]{0:T(1024)S(1)}, f32[768]{0:T(1024)}, u32[]{:S(2)}) copy-start(f32[768]{0:T(1024)} %param.29) | copy-start | bytes 9220
  74.0 0.9 copy-start.16
  74.0 2.0 copy-start.7
  78.8 2.4 copy-start.4
  78.8 2.4 copy-start.17
  81.2 1.9 copy-start.8
  83.0 39.3 %copy-start.9 = (f32[768]{0:T(1024)S(1)}, f32[768]{0:T(1024)}, u32[]{:S(2)}) copy-start(f32[768]{0:T(1024)} %param.34) | copy-start | bytes 9220
  83.1 142.8 %all-gather.7.cloned.1.call-start = ((), (), s32[]{:S(2)}) async-start(), calls=%async_computation.5 | async-start | bytes 4915200 | tf_op jit(solution)/shard_map/all_gather | solution.py:128
  119.6 2.8 %copy-start.2 = (bf16[8,256,768]{2,1,0:T(8,128)(2,1)S(1)}, bf16[8,256,768]{2,1,0:T(8,128)(2,1)}, u32[]{:S(2)}) copy-start(bf16[8,256,768]{2,1,0:T(8,128)(2,1)} %all-gather.5.cloned.1.call-done) | copy-start | bytes 9437188
  165.1 18.9 %copy-start.6 = (f32[768,32]{0,1:T(8,128)S(1)}, f32[768,32]{0,1:T(8,128)}, u32[]{:S(2)}) copy-start(f32[768,32]{0,1:T(8,128)} %param.35) | copy-start | bytes 294916
  225.9 13.2 %copy-start.1 = (bf16[8,128,768]{2,1,0:T(8,128)(2,1)S(1)}, bf16[8,128,768]{2,1,0:T(8,128)(2,1)}, u32[]{:S(2)}) copy-start(bf16[8,128,768]{2,1,0:T(8,128)(2,1)} %param.20) | copy-start | bytes 4718596
Sparse Core Ops, SparseCore 0:
  9.0 59.2 all-gather.8
  83.2 36.3 all-gather.4
  184.1 41.7 all-gather.6

commit v2 on v1

--- a/solution.py
+++ b/solution.py
@@ -1,6 +1,9 @@
+import functools
 import jax
 import jax.numpy as jnp
 from jax import lax
+from jax.experimental import pallas as pl
+from jax.experimental.pallas import tpu as pltpu
 from jax.sharding import PartitionSpec as P
 
 EPSILON = 1e-6
@@ -49,6 +52,185 @@
     return (jnp.sum(counts * one_hot.astype(jnp.float32), axis=-1) - 1.0).astype(jnp.int32)
 
 
+MESH_ID = pl.DeviceIdType.MESH
+
+
+def expert_kernel(ep_size, tp_size, send_ref, states_ref, code_ref, gate_ref, w_in_ref, w_out_ref, out_ref, w_in_buf, w_out_buf, recv_buf, hidden_buf, out_buf, slot_buf, w_sem, disp_send, disp_recv, back_send, back_recv, near_send, near_recv, far_send, far_recv):
+    me = lax.axis_index('ep')
+    row = lax.axis_index('tp')
+    chips = ep_size // 2
+    chip = me // 2
+    partner = me + 1 - 2 * (me % 2)
+    above = (row + 1) % tp_size
+    below = (row + tp_size - 1) % tp_size
+    across = (row + 2) % tp_size
+    capacity, d_model = send_ref.shape[1], send_ref.shape[2]
+    d_ff = w_in_buf.shape[1]
+    pair = 2 * capacity
+    tokens = states_ref.shape[0]
+
+    def weight_copies():
+        return (pltpu.make_async_copy(w_in_ref.at[row], w_in_buf, w_sem.at[0]),
+                pltpu.make_async_copy(w_out_ref.at[row], w_out_buf, w_sem.at[1]))
+
+    copy_in, copy_out = weight_copies()
+    copy_in.start()
+    copy_out.start()
+
+    barrier = pltpu.get_barrier_semaphore()
+    for step in range(1, ep_size):
+        pl.semaphore_signal(barrier, inc=1, device_id={'ep': (me + step) % ep_size}, device_id_type=MESH_ID)
+    for neighbour in (above, below):
+        pl.semaphore_signal(barrier, inc=1, device_id={'tp': neighbour}, device_id_type=MESH_ID)
+    pl.semaphore_wait(barrier, ep_size + 1)
+
+    def peers(relative):
+        if relative == 0:
+            return (partner,)
+        first = 2 * ((chip + relative) % chips)
+        return (first, first + 1)
+
+    def dispatch_copy(peer, source):
+        return pltpu.make_async_remote_copy(
+            src_ref=send_ref.at[peer], dst_ref=recv_buf.at[source], send_sem=disp_send.at[peer], recv_sem=disp_recv.at[source],
+            device_id={'ep': peer}, device_id_type=MESH_ID)
+
+    def back_copy(peer, source):
+        return pltpu.make_async_remote_copy(
+            src_ref=out_buf.at[peer], dst_ref=slot_buf.at[row, source], send_sem=back_send.at[peer], recv_sem=back_recv.at[source],
+            device_id={'ep': peer}, device_id_type=MESH_ID)
+
+    def near_copy(relative, holder, side, target):
+        block = 2 * ((chip + relative) % chips)
+        return pltpu.make_async_remote_copy(
+            src_ref=slot_buf.at[holder, pl.ds(block, 2)], dst_ref=slot_buf.at[holder, pl.ds(block, 2)],
+            send_sem=near_send.at[relative, side], recv_sem=near_recv.at[relative, side],
+            device_id={'tp': target}, device_id_type=MESH_ID)
+
+    def far_copy(relative, holder, side, target):
+        block = 2 * ((chip + relative) % chips) + side
+        return pltpu.make_async_remote_copy(
+            src_ref=slot_buf.at[holder, block], dst_ref=slot_buf.at[holder, block],
+            send_sem=far_send.at[relative, side], recv_sem=far_recv.at[relative, side],
+            device_id={'tp': target}, device_id_type=MESH_ID)
+
+    compute_order = (0, 1, chips - 1, 2)
+    back_order = (0, chips - 1, 1, 2)
+    for relative in compute_order:
+        for peer in peers(relative):
+            dispatch_copy(peer, me).start()
+    recv_buf[me] = send_ref[me]
+    out_ref[...] = states_ref[...]
+
+    def compute(relative):
+        for peer in peers(relative):
+            dispatch_copy(peer, peer).wait_recv()
+        if relative == 0:
+            copy_in.wait()
+        block = 2 * ((chip + relative) % chips)
+        inputs = recv_buf[pl.ds(block, 2)].reshape(pair, d_model)
+        width = d_ff // 4
+
+        def first(step, carry):
+            columns = pl.ds(pl.multiple_of(step * width, width), width)
+            hidden = jnp.dot(inputs, w_in_buf[:, columns], preferred_element_type=jnp.float32)
+            hidden_buf[:, columns] = jnp.maximum(hidden, 0.0).astype(jnp.bfloat16)
+            return carry
+
+        lax.fori_loop(0, 4, first, 0)
+        if relative == 0:
+            copy_out.wait()
+        result = jnp.dot(hidden_buf[...], w_out_buf[...], preferred_element_type=jnp.float32).astype(jnp.bfloat16)
+        out_buf[pl.ds(block, 2)] = result.reshape(2, capacity, d_model)
+        if relative == 0:
+            slot_buf[row, me] = out_buf[me]
+        for peer in peers(relative):
+            back_copy(peer, me).start()
+
+    def share(relative):
+        for peer in peers(relative):
+            back_copy(peer, peer).wait_recv()
+        near_copy(relative, row, 0, above).start()
+        near_copy(relative, row, 1, below).start()
+
+    def forward(relative):
+        near_copy(relative, below, 0, above).wait_recv()
+        far_copy(relative, below, 0, above).start()
+        near_copy(relative, above, 1, below).wait_recv()
+        far_copy(relative, above, 1, below).start()
+
+    def combine(relative):
+        far_copy(relative, across, 0, above).wait_recv()
+        far_copy(relative, across, 1, below).wait_recv()
+        which = (chip + relative) % chips
+        values = jnp.concatenate([slot_buf[holder, pl.ds(2 * which, 2)].reshape(pair, d_model) for holder in range(tp_size)], axis=0)
+        tile = 256
+
+        def body(step, carry):
+            rows = pl.ds(pl.multiple_of(step * tile, tile), tile)
+            wanted = code_ref[rows, :] - which * (tp_size * pair)
+            pick = (wanted == lax.broadcasted_iota(jnp.int32, (tile, tp_size * pair), 1)).astype(jnp.float32).astype(jnp.bfloat16)
+            picked = jnp.dot(pick, values, preferred_element_type=jnp.float32)
+            out_ref[rows, :] = (out_ref[rows, :].astype(jnp.float32) + gate_ref[rows, :] * picked).astype(jnp.bfloat16)
+            return carry
+
+        lax.fori_loop(0, tokens // tile, body, 0)
+
+    near_1, near_2, near_3 = back_order[1:]
+    compute(compute_order[0])
+    share(0)
+    compute(compute_order[1])
+    compute(compute_order[2])
+    share(near_1)
+    forward(0)
+    compute(compute_order[3])
+    share(near_2)
+    forward(near_1)
+    combine(0)
+    share(near_3)
+    forward(near_2)
+    combine(near_1)
+    forward(near_3)
+    combine(near_2)
+    combine(near_3)
+
+    for relative in compute_order:
+        for peer in peers(relative):
+            dispatch_copy(peer, me).wait_send()
+            back_copy(peer, me).wait_send()
+        near_copy(relative, row, 0, above).wait_send()
+        near_copy(relative, row, 1, below).wait_send()
+        far_copy(relative, below, 0, above).wait_send()
+        far_copy(relative, above, 1, below).wait_send()
+
+
+def expert_exchange(send_buf, states, code, gate, w_in, w_out, ep_size, tp_size):
+    capacity, d_model = send_buf.shape[1], send_buf.shape[2]
+    d_ff = w_in.shape[2]
+    vmem = pl.BlockSpec(memory_space=pltpu.VMEM)
+    anywhere = pl.BlockSpec(memory_space=pl.ANY)
+    dma = pltpu.SemaphoreType.DMA
+    chips = ep_size // 2
+    return pl.pallas_call(
+        functools.partial(expert_kernel, ep_size, tp_size),
+        out_shape=jax.ShapeDtypeStruct(states.shape, jnp.bfloat16),
+        in_specs=[vmem, vmem, vmem, vmem, anywhere, anywhere],
+        out_specs=vmem,
+        scratch_shapes=[
+            pltpu.VMEM((d_model, d_ff), jnp.bfloat16),
+            pltpu.VMEM((d_ff, d_model), jnp.bfloat16),
+            pltpu.VMEM((ep_size, capacity, d_model), jnp.bfloat16),
+            pltpu.VMEM((2 * capacity, d_ff), jnp.bfloat16),
+            pltpu.VMEM((ep_size, capacity, d_model), jnp.bfloat16),
+            pltpu.VMEM((tp_size, ep_size, capacity, d_model), jnp.bfloat16),
+            dma((2,)), dma((ep_size,)), dma((ep_size,)), dma((ep_size,)), dma((ep_size,)),
+            dma((chips, 2)), dma((chips, 2)), dma((chips, 2)), dma((chips, 2)),
+        ],
+        compiler_params=pltpu.CompilerParams(collective_id=0, has_side_effects=True),
+        name='expert_exchange',
+    )(send_buf, states, code, gate, w_in, w_out)
+
+
 def solution(mesh):
     ep_size = mesh.shape['ep']
     tp_size = mesh.shape['tp']
@@ -103,36 +285,28 @@
         tokens = batch_dev * dec_len
         experts = w_router.shape[1]
         capacity = (5 * tokens + 4 * experts - 1) // (4 * experts)
-        row_cap = -(-capacity // tp_size)
-        slots = experts * row_cap
+        local_experts = experts // ep_size
+        assert local_experts == tp_size
         choice = expert_idx.reshape(tokens)
         position = token_positions(choice, experts)
         kept = position < capacity
-        slot_row = position // row_cap
-        local_slot = choice * row_cap + position % row_cap
-        slot_here = jnp.where(kept & (slot_row == tp_id), local_slot, -1)
-        slot_full = jnp.where(kept, slot_row * slots + local_slot, -1)
+        owner = choice // local_experts
+        owner_row = choice % local_experts
+        slots = ep_size * capacity
+        slot_here = jnp.where(kept & (owner_row == tp_id), owner * capacity + position, -1)
+        pair_slots = 2 * capacity
+        code = (owner // 2) * (tp_size * pair_slots) + owner_row * pair_slots + (owner % 2) * capacity + position
+        code = jnp.where(kept, code, -1)
 
         states = after_cross.reshape(tokens, d_model)
         normed = rms_norm(states, gain_ffn)
         dispatch = (lax.broadcasted_iota(jnp.int32, (slots, tokens), 0) == slot_here[None, :]).astype(jnp.bfloat16)
-        send_buf = matmul_f32(dispatch, normed).astype(jnp.bfloat16)
-        local_experts = experts // ep_size
-        received = lax.all_to_all(send_buf.reshape(ep_size, local_experts * row_cap, d_model), 'ep', 0, 0, tiled=True)
-        received = received.reshape(ep_size, local_experts, row_cap, d_model)
-        received = jnp.transpose(received, (1, 0, 2, 3)).reshape(local_experts, ep_size * row_cap, d_model)
-        hidden = jnp.maximum(jnp.einsum('ecd,edf->ecf', received, w_in, preferred_element_type=jnp.float32), 0.0).astype(jnp.bfloat16)
-        expert_out = jnp.einsum('ecf,efd->ecd', hidden, w_out, preferred_element_type=jnp.float32).astype(jnp.bfloat16)
-        expert_out = jnp.transpose(expert_out.reshape(local_experts, ep_size, row_cap, d_model), (1, 0, 2, 3))
-        returned = lax.all_to_all(expert_out.reshape(ep_size, local_experts * row_cap, d_model), 'ep', 0, 0, tiled=True)
-        all_slots = lax.all_gather(returned.reshape(slots, d_model), 'tp', axis=0, tiled=True)
+        send_buf = matmul_f32(dispatch, normed).astype(jnp.bfloat16).reshape(ep_size, capacity, d_model)
 
         logits = sum(matmul_f32(normed, piece) for piece in split_three(w_router))
         router_prob = jax.nn.softmax(logits, axis=-1)
         gate_prob = jnp.sum(jnp.where(choice[:, None] == lax.broadcasted_iota(jnp.int32, (tokens, experts), 1), router_prob, 0.0), axis=-1)
-        pick = (slot_full[:, None] == lax.broadcasted_iota(jnp.int32, (tokens, tp_size * slots), 1)).astype(jnp.bfloat16)
-        combined = matmul_f32(pick, all_slots)
-        result = states.astype(jnp.float32) + gate_prob[:, None] * combined
-        return result.astype(jnp.bfloat16).reshape(batch_dev, dec_len, d_model)
+        result = expert_exchange(send_buf, states, code[:, None], gate_prob[:, None], w_in, w_out, ep_size, tp_size)
+        return result.reshape(batch_dev, dec_len, d_model)
 
     return jax.shard_map(layer, mesh=mesh, in_specs=in_specs, out_specs=token_spec, check_vma=False)

time: 246 us -> 203 us (0.83)
  Pallas kernels: 0 us -> 60.5 us
  waiting for transfers between devices: 93.7 us -> 51.3 us
  blocking collectives: 37.6 us -> 0 us
  matrix products: 65.1 us -> 36.8 us
  other arithmetic: 10.9 us -> 13.9 us
    pallas_call x0 -> x1, Pallas kernels: none -> 60.5 us  [expert_exchange(): pl.pallas_call(functools.partial(expert_kernel, ep_size, tp_size), out_sh...]
    all_gather x1 -> x0, waiting for transfers between devices: 38.7 us -> none  [layer(): lax.all_gather(returned.reshape(slots, d_model), 'tp', axis=0, tiled=True)]
    all_to_all x2 -> x0, blocking collectives: 37.6 us -> none  [the longest x1 19.3 us: layer(): lax.all_to_all(send_buf.reshape(ep_size, local_experts * row_cap, d_model...]
    dot_general x1 -> x0, matrix products: 16.3 us -> none  [layer(): jnp.einsum('ecf,efd->ecd', hidden, w_out, preferred_element_type=jnp.floa...]
    dot_general x12 -> x11, matrix products: 31.8 us -> 19.7 us  [matmul_f32(): return jnp.dot(left, right, preferred_element_type=jnp.float32)]
    unnamed x38 -> x41, local copies, waits for them, and re-layouts: 1.06 us -> 5.37 us
    all_gather x1, waiting for transfers between devices: 35.2 us -> 31.5 us  [layer(): after_cross = lax.all_gather(after_cross, 'tp', axis=0, tiled=True)]
    select_n x2, other arithmetic: 0.04 us -> 3.02 us  [the longest x1 3 us: layer(): code = jnp.where(kept, code, -1)]
  transfers between devices with their start and end apart: 5 -> 4, of which waited for: 3 -> 2; matrix products, arithmetic and copies ran while one was open for 15% -> 18% of each run, Pallas kernels for 0% -> 0%
where the time goes in v2:
time: 203 us
  Pallas kernels  60.5 us (30%)
  waiting for transfers between devices  51.3 us (25%)
  matrix products  36.8 us (18%)
  local copies, waits for them, and re-layouts  15.3 us (8%)
  other arithmetic  13.9 us (7%)
  between operations  13.8 us (7%)
  starting transfers between devices  11.1 us (5%)
    pallas_call x1, Pallas kernels, expert_exchange(): pl.pallas_call(functools.partial(expert_kernel, ep_size, tp_size), out_sh...  60.5 us
    all_gather x1, waiting for transfers between devices, layer(): after_cross = lax.all_gather(after_cross, 'tp', axis=0, tiled=True)  31.5 us
    dot_general x11, matrix products, matmul_f32(): return jnp.dot(left, right, preferred_element_type=jnp.float32)  19.7 us
    all_gather x1, waiting for transfers between devices, layer(): w_all = lax.all_gather(w_pack, 'tp', axis=0, tiled=False)  19.6 us
    sub x2, matrix products, attention_context(): weights = jax.nn.softmax(scores, axis=-1).astype(jnp.bfloat16)  9.06 us
    dot_general x2, matrix products, attention_context(): jnp.einsum('bhqk,bkhe->bqhe', weights, values, preferred_element_type=jnp...  6.98 us
    all_to_all x1, starting transfers between devices, layer(): lax.all_to_all(kv_local.reshape(tp_size, own_batch, -1, 2 * width), 'tp',...  6.6 us
    unnamed x41, local copies, waits for them, and re-layouts  5.37 us
  transfers between devices with their start and end apart: 4, of which 2 were waited for; matrix products, arithmetic and copies ran while one was open for 18% of the time, Pallas kernels for 0%

profile of v2, /device:TPU:97, one launch (start us, length us, event | category | flops | bytes accessed | tf_op | source)
XLA Modules:
  0.0 202.7 jit_solution(7803707634731275280)
XLA Ops:
  6.6 2.2 %pad_maximum_fusion = bf16[576,768]{1,0:T(8,128)(2,1)} fusion(bf16[192,768]{1,0:T(8,128)(2,1)} %bitcast.128, bf16[192,768]{1,0:T(8,128)(2,1)} %param.33, bf16[192,768]{1,0:T(8,128)(2,1)} %param.28), kind=kLoop, calls=%fused_computation.76 | loop fusion | flops 2654208 | bytes 1769472 | tf_op jit(solution)/shard_map/concatenate | solution.py:252
  8.8 0.1 all-gather.6.cloned.1.call-update
  8.9 1.6 convolution_convert_fusion.2
  10.5 0.7 convolution_convert_fusion.1
  11.2 0.0 copy-start.3
  11.2 0.9 pad_maximum_fusion.1
  12.1 6.6 %all-to-all-start.1 = ((bf16[4,2,128,384]{2,3,1,0:T(8,128)(2,1)}), bf16[4,2,128,384]{2,3,1,0:T(8,128)(2,1)}, u32[]{:S(2)}, u32[]{:S(2)}) async-start(bf16[4,2,128,384]{2,3,1,0:T(8,128)(2,1)} %pad_maximum_fusion.1), calls=%async_computation.1 | async-start | bytes 1572864 | tf_op jit(solution)/shard_map/all_to_all | solution.py:259
  18.8 0.0 copy-start.11
  18.8 0.0 copy-start.14
  18.8 2.1 %broadcast_select_fusion = f32[3,256,256]{2,1,0:T(8,128)} fusion(f32[3,256,256]{2,1,0:T(8,128)} %param.23, pred[256,256]{1,0:T(8,128)(4,1)S(1)} %iota_compare_fusion.5), kind=kLoop, calls=%fused_computation.81 | loop fusion | flops 196608 | bytes 1638400 | tf_op jit(solution)/shard_map/jit(_where)/select_n | solution.py:263
  20.9 2.3 %copy.64 = f32[3,256,256]{1,2,0:T(8,128)} copy(f32[3,256,256]{2,1,0:T(8,128)} %broadcast_select_fusion) | data formatting | bytes 1572864 | tf_op jit(solution)/shard_map/jit(_where)/select_n | solution.py:263
  23.2 0.7 fusion.2
  23.9 0.0 copy-done.11
  23.9 0.0 copy-done.14
  23.9 0.0 copy-start.12
  23.9 2.2 %fusion.32 = bf16[8,256,192]{1,2,0:T(8,128)(2,1)} fusion(bf16[8,256,768]{2,1,0:T(8,128)(2,1)S(1)} %copy-done.3, f32[768]{0:T(1024)S(1)} %copy-done.14, f32[8,256]{1,0:T(8,128)S(1)} %add_rsqrt_fusion, bf16[768,192]{0,1:T(8,128)(2,1)S(1)} %copy-done.11), kind=kOutput, calls=%fused_computation.50 | convolution fusion | flops 610664448 | bytes 4238336 | tf_op jit(solution)/shard_map/dot_general | solution.py:20
  26.1 2.2 %fusion.35 = bf16[8,256,192]{1,2,0:T(8,128)(2,1)} fusion(bf16[8,256,768]{2,1,0:T(8,128)(2,1)S(1)} %copy-done.3, f32[768]{0:T(1024)S(1)} %copy-done.14, f32[8,256]{1,0:T(8,128)S(1)} %add_rsqrt_fusion, bf16[768,192]{0,1:T(8,128)(2,1)S(1)} %copy-done.12), kind=kOutput, calls=%fused_computation.51 | convolution fusion | flops 610664448 | bytes 4238336 | tf_op jit(solution)/shard_map/dot_general | solution.py:20
  28.3 2.2 %fusion.29 = bf16[8,256,192]{1,2,0:T(8,128)(2,1)} fusion(bf16[8,256,768]{2,1,0:T(8,128)(2,1)S(1)} %copy-done.3, f32[768]{0:T(1024)S(1)} %copy-done.14, f32[8,256]{1,0:T(8,128)S(1)} %add_rsqrt_fusion, bf16[768,192]{0,1:T(8,128)(2,1)S(1)} %copy-done.13), kind=kOutput, calls=%fused_computation.49 | convolution fusion | flops 610664448 | bytes 4238336 | tf_op jit(solution)/shard_map/dot_general | solution.py:20
  30.5 6.3 %fusion.84 = (f32[8,3,256]{2,1,0:T(4,128)S(1)}, f32[8,3,256,256]{2,3,1,0:T(8,128)}) fusion(f32[3,256,256]{1,2,0:T(8,128)} %copy.64, bf16[8,256,3,64]{1,3,2,0:T(8,128)(2,1)} %bitcast.138, bf16[8,256,3,64]{1,3,2,0:T(8,128)(2,1)} %bitcast.139), kind=kOutput, calls=%fused_computation.126 | convolution fusion | flops 206045440 | bytes 8675328 | tf_op jit(solution)/shard_map/sub | solution.py:29
  36.8 4.6 %fusion.39 = bf16[8,3,64,256]{3,2,1,0:T(8,128)(2,1)} fusion(bf16[8,256,3,64]{1,3,2,0:T(8,128)(2,1)} %bitcast.137, f32[8,3,256,256]{2,3,1,0:T(8,128)} %get-tuple-element.10, f32[8,3,256]{2,1,0:T(4,128)S(1)} %get-tuple-element.9), kind=kOutput, calls=%fused_computation.54 | convolution fusion | flops 204865536 | bytes 7888896 | tf_op jit(solution)/shard_map/bhqk,bkhe->bqhe/dot_general | solution.py:30
  41.4 0.0 all-to-all-done.1
  41.4 4.3 %all-to-all-start = ((bf16[8,256,192]{1,2,0:T(8,128)(2,1)}), bf16[8,256,192]{1,2,0:T(8,128)(2,1)}, u32[]{:S(2)}, u32[]{:S(2)}) async-start(bf16[8,256,192]{1,2,0:T(8,128)(2,1)} %bitcast.122), calls=%async_computation | async-start | bytes 1572864 | tf_op jit(solution)/shard_map/all_to_all | solution.py:269
  45.7 0.2 all-gather.4.cloned.1.call-start
  45.9 0.7 compare_select_fusion
  46.6 1.2 fusion.83
  47.8 0.8 copy.68
  48.6 19.6 %all-gather.6.cloned.1.call-done = bf16[2304,768]{1,0:T(8,128)(2,1)} async-done(((bf16[576,768]{1,0:T(8,128)(2,1)}), bf16[2304,768]{1,0:T(8,128)(2,1)}) %all-gather.6.cloned.1.call-update) | async-done | bytes 3538960 | tf_op jit(solution)/shard_map/all_gather | solution.py:253
  68.3 3.2 %fusion.82 = (bf16[4,192,768]{2,1,0:T(8,128)(2,1)}, bf16[4,192,768]{2,1,0:T(8,128)(2,1)}) fusion(bf16[4,576,768]{2,1,0:T(8,128)(2,1)} %bitcast.117), kind=kLoop, calls=%fused_computation.124 | loop fusion | bytes 4718592 | tf_op jit(solution)/shard_map/slice | solution.py:255
  71.4 0.0 all-to-all-done
  71.5 2.5 %fusion.21 = (f32[2,256]{1,0:T(2,128)S(1)}, bf16[2,256,768]{2,1,0:T(8,128)(2,1)S(1)}) fusion(bf16[2,256,4,192]{1,3,0,2:T(8,128)(2,1)} %bitcast.12, bf16[4,576,768]{2,1,0:T(8,128)(2,1)} %bitcast.118, bf16[8,256,768]{2,1,0:T(8,128)(2,1)S(1)} %copy-done.3, s32[]{:T(128)S(6)} %select_n.96), kind=kOutput, calls=%fused_computation.30 | convolution fusion | flops 606338560 | bytes 3540996 | tf_op jit(solution)/shard_map/dot_general | solution.py:20
  74.0 0.9 copy-done.16
  74.9 0.0 copy-done.15
  74.9 0.8 convolution_convert_fusion
  75.8 0.3 copy.67
  76.1 2.8 %fusion.85 = (f32[2,12,256]{2,1,0:T(8,128)S(1)}, f32[2,12,256,128]{2,3,1,0:T(8,128)}) fusion(f32[2,128]{1,0:T(2,128)S(1)} %compare_select_fusion, bf16[2,256,12,64]{1,3,2,0:T(8,128)(2,1)S(1)} %bitcast.123, bf16[2,128,12,64]{1,3,2,0:T(8,128)(2,1)S(1)} %bitcast.125), kind=kOutput, calls=%fused_computation.127 | convolution fusion | flops 103022720 | bytes 4350976 | tf_op jit(solution)/shard_map/sub | solution.py:29
  78.8 2.4 %fusion.38 = bf16[2,12,64,256]{3,2,1,0:T(8,128)(2,1)S(1)} fusion(bf16[2,128,12,64]{1,3,2,0:T(8,128)(2,1)S(1)} %bitcast.124, f32[2,12,256,128]{2,3,1,0:T(8,128)} %get-tuple-element.14, f32[2,12,256]{2,1,0:T(8,128)S(1)} %get-tuple-element.13), kind=kOutput, calls=%fused_computation.53 | convolution fusion | flops 102629376 | bytes 4349952 | tf_op jit(solution)/shard_map/bhqk,bkhe->bqhe/dot_general | solution.py:30
  81.2 0.0 copy-start.8
  81.3 1.7 fusion.24
  83.0 0.1 all-gather.4.cloned.1.call-update
  83.1 0.2 convolution_bitcast_fusion
  83.3 0.1 slice.24
  83.4 0.2 copy.62
  83.6 0.2 copy.63
  83.8 0.3 subtract_reduce_fusion
  84.1 0.1 multiply_reduce_fusion.1
  84.2 0.4 copy.71
  84.6 0.4 copy.87
  85.0 0.0 copy-start.9
  85.0 3.0 %fusion.44.code_ref = s32[2048,1]{1,0:T(8,128)} fusion(s32[2048,1]{1,0:T(8,128)S(1)} %copy.71, s32[1,2048]{0,1:T(8,128)S(1)} %copy.87), kind=kLoop, calls=%fused_computation.63 | loop fusion | flops 94208 | bytes 24576 | tf_op jit(solution)/shard_map/jit(_where)/select_n | solution.py:299
  88.0 31.5 %all-gather.4.cloned.1.call-done = bf16[8,256,768]{2,1,0:T(8,128)(2,1)} async-done(((bf16[2,256,768]{2,1,0:T(8,128)(2,1)}), bf16[8,256,768]{2,1,0:T(8,128)(2,1)}) %all-gather.4.cloned.1.call-update) | async-done | bytes 3145744 | tf_op jit(solution)/shard_map/all_gather | solution.py:283
  119.6 2.7 %multiply_reduce_fusion = f32[8,256]{1,0:T(8,128)S(1)} fusion(bf16[8,256,768]{2,1,0:T(8,128)(2,1)} %all-gather.4.cloned.1.call-done), kind=kLoop, calls=%fused_computation.8 | loop fusion | flops 4716544 | bytes 3153920 | tf_op jit(solution)/shard_map/reduce_sum | solution.py:15
  122.3 0.1 copy-done.2
  122.4 0.8 multiply_convert_fusion
  123.2 0.1 copy-done.6
  123.3 1.0 fusion.70
  124.3 1.0 convolution_add_fusion.1
  125.3 1.1 fusion.86
  126.4 0.1 fusion.67
  126.4 0.1 select_reduce_fusion
  126.5 1.4 copy.79.gate_ref
  127.9 3.6 %fusion.28 = bf16[640,768]{1,0:T(8,128)(2,1)} fusion(bf16[2048,768]{1,0:T(8,128)(2,1)S(1)} %multiply_convert_fusion, s32[2048]{0:T(1024)S(1)} %fusion.78), kind=kOutput, calls=%fused_computation.48 | convolution fusion | flops 2015068160 | bytes 4136960 | tf_op jit(solution)/shard_map/dot_general | solution.py:20
  131.5 60.5 %expert_exchange.1 = bf16[2048,768]{1,0:T(8,128)(2,1)} custom-call(bf16[8,80,768]{2,1,0:T(8,128)(2,1)} %bitcast.121, bf16[2048,768]{1,0:T(8,128)(2,1)} %bitcast.115, s32[2048,1]{1,0:T(8,128)} %fusion.44.code_ref, f32[2048,1]{1,0:T(8,128)} %copy.79.gate_ref, bf16[4,768,3072]{2,1,0:T(8,128)(2,1)} %w_in_ref.1, bf16[4,3072,768]{2,1,0:T(8,128)(2,1)} %w_out_ref.1), custom_call_target="tpu_custom_call" | custom-call | tf_op jit(solution)/shard_map/expert_exchange/pallas_call | solution.py:214
  192.0 0.0 copy-start.1
  192.0 3.9 %copy.89 = bf16[8,256,768]{2,1,0:T(8,128)(2,1)} copy(bf16[8,256,768]{2,1,0:T(8,128)(2,1)} %bitcast.116) | data formatting | bytes 6291456
  (36 shorter events, 0.2 us)
Async XLA Ops:
  6.5 2.3 %copy-start = (bf16[8,128,768]{2,1,0:T(8,128)(2,1)S(1)}, bf16[8,128,768]{2,1,0:T(8,128)(2,1)}, u32[]{:S(2)}) copy-start(bf16[8,128,768]{2,1,0:T(8,128)(2,1)} %param.20) | copy-start | bytes 4718596
  6.6 4.0 %copy-start.10 = (bf16[768,192]{0,1:T(8,128)(2,1)S(1)}, bf16[768,192]{0,1:T(8,128)(2,1)}, u32[]{:S(2)}) copy-start(bf16[768,192]{0,1:T(8,128)(2,1)} %param.32) | copy-start | bytes 884740
  6.6 61.7 %all-gather.6.cloned.1.call-start = ((), (), s32[]{:S(2)}) async-start(), calls=%async_computation.3 | async-start | bytes 4423680 | tf_op jit(solution)/shard_map/all_gather | solution.py:253
  11.2 12.0 %copy-start.3 = (bf16[8,256,768]{2,1,0:T(8,128)(2,1)S(1)}, bf16[8,256,768]{2,1,0:T(8,128)(2,1)}, u32[]{:S(2)}) copy-start(bf16[8,256,768]{2,1,0:T(8,128)(2,1)} %param.19) | copy-start | bytes 9437188
  12.1 29.2 %all-to-all-start.1 = ((bf16[4,2,128,384]{2,3,1,0:T(8,128)(2,1)}), bf16[4,2,128,384]{2,3,1,0:T(8,128)(2,1)}, u32[]{:S(2)}, u32[]{:S(2)}) async-start(bf16[4,2,128,384]{2,3,1,0:T(8,128)(2,1)} %pad_maximum_fusion.1), calls=%async_computation.1 | async-start | bytes 1572864 | tf_op jit(solution)/shard_map/all_to_all | solution.py:259
  18.8 5.1 %copy-start.11 = (bf16[768,192]{0,1:T(8,128)(2,1)S(1)}, bf16[768,192]{0,1:T(8,128)(2,1)}, u32[]{:S(2)}) copy-start(bf16[768,192]{0,1:T(8,128)(2,1)} %param.25) | copy-start | bytes 884740
  18.8 5.1 %copy-start.14 = (f32[768]{0:T(1024)S(1)}, f32[768]{0:T(1024)}, u32[]{:S(2)}) copy-start(f32[768]{0:T(1024)} %param.24) | copy-start | bytes 9220
  23.9 2.2 %copy-start.12 = (bf16[768,192]{0,1:T(8,128)(2,1)S(1)}, bf16[768,192]{0,1:T(8,128)(2,1)}, u32[]{:S(2)}) copy-start(bf16[768,192]{0,1:T(8,128)(2,1)} %param.26) | copy-start | bytes 884740
  26.1 2.2 %copy-start.13 = (bf16[768,192]{0,1:T(8,128)(2,1)S(1)}, bf16[768,192]{0,1:T(8,128)(2,1)}, u32[]{:S(2)}) copy-start(bf16[768,192]{0,1:T(8,128)(2,1)} %param.27) | copy-start | bytes 884740
  41.4 30.1 %all-to-all-start = ((bf16[8,256,192]{1,2,0:T(8,128)(2,1)}), bf16[8,256,192]{1,2,0:T(8,128)(2,1)}, u32[]{:S(2)}, u32[]{:S(2)}) async-start(bf16[8,256,192]{1,2,0:T(8,128)(2,1)} %bitcast.122), calls=%async_computation | async-start | bytes 1572864 | tf_op jit(solution)/shard_map/all_to_all | solution.py:269
  45.7 73.9 %all-gather.4.cloned.1.call-start = ((), (), s32[]{:S(2)}) async-start(), calls=%async_computation.2 | async-start | bytes 3932160 | tf_op jit(solution)/shard_map/all_gather | solution.py:283
  71.4 3.5 %copy-start.5 = (bf16[4,192,768]{2,1,0:T(8,128)(2,1)S(1)}, bf16[4,192,768]{2,1,0:T(8,128)(2,1)}, u32[]{:S(2)}) copy-start(bf16[4,192,768]{2,1,0:T(8,128)(2,1)} %get-tuple-element.6) | copy-start | bytes 3538948
  71.5 3.5 %copy-start.15 = (f32[768]{0:T(1024)S(1)}, f32[768]{0:T(1024)}, u32[]{:S(2)}) copy-start(f32[768]{0:T(1024)} %param.29) | copy-start | bytes 9220
  74.0 0.9 copy-start.16
  74.0 2.0 %copy-start.7 = (bf16[2,128,4,192]{1,3,2,0:T(8,128)(2,1)S(1)}, bf16[2,128,4,192]{1,3,2,0:T(8,128)(2,1)}, u32[]{:S(2)}) copy-start(bf16[2,128,4,192]{1,3,2,0:T(8,128)(2,1)} %copy.68) | copy-start | bytes 1179652
  78.8 2.4 %copy-start.4 = (bf16[4,192,768]{2,1,0:T(8,128)(2,1)S(1)}, bf16[4,192,768]{2,1,0:T(8,128)(2,1)}, u32[]{:S(2)}) copy-start(bf16[4,192,768]{2,1,0:T(8,128)(2,1)} %get-tuple-element.5) | copy-start | bytes 3538948
  78.8 2.4 %copy-start.17 = (bf16[2,256,768]{2,1,0:T(8,128)(2,1)S(1)}, bf16[2,256,768]{2,1,0:T(8,128)(2,1)}, u32[]{:S(2)}) copy-start(bf16[2,256,768]{2,1,0:T(8,128)(2,1)} %copy-done.16) | copy-start | bytes 2359300
  81.2 1.8 copy-start.8
  85.0 37.3 %copy-start.9 = (f32[768]{0:T(1024)S(1)}, f32[768]{0:T(1024)}, u32[]{:S(2)}) copy-start(f32[768]{0:T(1024)} %param.34) | copy-start | bytes 9220
  119.6 2.8 %copy-start.2 = (bf16[8,256,768]{2,1,0:T(8,128)(2,1)S(1)}, bf16[8,256,768]{2,1,0:T(8,128)(2,1)}, u32[]{:S(2)}) copy-start(bf16[8,256,768]{2,1,0:T(8,128)(2,1)} %all-gather.4.cloned.1.call-done) | copy-start | bytes 9437188
  122.4 0.9 copy-start.6
  192.0 3.9 %copy-start.1 = (bf16[8,128,768]{2,1,0:T(8,128)(2,1)S(1)}, bf16[8,128,768]{2,1,0:T(8,128)(2,1)}, u32[]{:S(2)}) copy-start(bf16[8,128,768]{2,1,0:T(8,128)(2,1)} %param.20) | copy-start | bytes 4718596
Sparse Core Ops, SparseCore 0:
  9.0 59.2 all-gather.5
  83.2 36.3 all-gather.3

commit v3 on v2

--- a/solution.py
+++ b/solution.py
@@ -55,7 +55,7 @@
 MESH_ID = pl.DeviceIdType.MESH
 
 
-def expert_kernel(ep_size, tp_size, send_ref, states_ref, code_ref, gate_ref, w_in_ref, w_out_ref, out_ref, w_in_buf, w_out_buf, recv_buf, hidden_buf, out_buf, slot_buf, w_sem, disp_send, disp_recv, back_send, back_recv, near_send, near_recv, far_send, far_recv):
+def expert_kernel(ep_size, tp_size, capacity, experts, own_ref, slot_ref, code_ref, gain_ref, route_ref, w_in_ref, w_out_ref, out_ref, w_in_buf, w_out_buf, states_buf, gate_buf, send_ref, recv_buf, hidden_buf, out_buf, slot_buf, w_sem, part_send, part_recv, rest_send, rest_recv, disp_send, disp_recv, back_send, back_recv, near_send, near_recv, far_send, far_recv):
     me = lax.axis_index('ep')
     row = lax.axis_index('tp')
     chips = ep_size // 2
@@ -64,10 +64,12 @@
     above = (row + 1) % tp_size
     below = (row + tp_size - 1) % tp_size
     across = (row + 2) % tp_size
-    capacity, d_model = send_ref.shape[1], send_ref.shape[2]
+    own_batch, dec_len, d_model = own_ref.shape
     d_ff = w_in_buf.shape[1]
     pair = 2 * capacity
-    tokens = states_ref.shape[0]
+    tokens = code_ref.shape[0]
+    slots = ep_size * capacity
+    lanes = 128
 
     def weight_copies():
         return (pltpu.make_async_copy(w_in_ref.at[row], w_in_buf, w_sem.at[0]),
@@ -114,13 +116,74 @@
             send_sem=far_send.at[relative, side], recv_sem=far_recv.at[relative, side],
             device_id={'tp': target}, device_id_type=MESH_ID)
 
+    def part_copy(holder, part, side, target):
+        source = own_ref.at[part] if holder is row else states_buf.at[holder, part]
+        return pltpu.make_async_remote_copy(
+            src_ref=source, dst_ref=states_buf.at[holder, part], send_sem=part_send.at[part, side], recv_sem=part_recv.at[part, side],
+            device_id={'tp': target}, device_id_type=MESH_ID)
+
+    def rest_copy(holder, side, target):
+        return pltpu.make_async_remote_copy(
+            src_ref=states_buf.at[holder, side], dst_ref=states_buf.at[holder, side], send_sem=rest_send.at[side], recv_sem=rest_recv.at[side],
+            device_id={'tp': target}, device_id_type=MESH_ID)
+
+    part_copy(row, 0, 0, above).start()
+    part_copy(row, 1, 1, below).start()
+    part_copy(row, 1, 0, above).start()
+    part_copy(row, 0, 1, below).start()
+    states_buf[row] = own_ref[...]
+    lane_ids = lax.broadcasted_iota(jnp.int32, (1, lanes), 1)
+    local = experts // ep_size
+    owner = lane_ids // local
+    base = (owner // 2) * (tp_size * pair) + (lane_ids % local) * pair + (owner % 2) * capacity
+
+    def absorb(holder, part, fresh):
+        block = holder * own_batch + part
+        upcast = states_buf[holder, part].astype(jnp.float32)
+        mean_sq = jnp.mean(upcast * upcast, axis=-1, keepdims=True)
+        normed = (upcast * lax.rsqrt(mean_sq + EPSILON) * gain_ref[...]).astype(jnp.bfloat16)
+        wanted = slot_ref[block]
+        pick = (wanted == lax.broadcasted_iota(jnp.int32, (slots, dec_len), 0)).astype(jnp.float32).astype(jnp.bfloat16)
+        picked = jnp.dot(pick, normed, preferred_element_type=jnp.float32).astype(jnp.bfloat16).reshape(ep_size, capacity, d_model)
+        if fresh:
+            send_ref[...] = picked
+        else:
+            send_ref[...] = send_ref[...] + picked
+        parts = jnp.dot(normed, route_ref[...], preferred_element_type=jnp.float32)
+        logits = parts[:, :lanes] + parts[:, lanes:2 * lanes] + parts[:, 2 * lanes:]
+        logits = jnp.where(lane_ids < experts, logits, NEG_LARGE)
+        powers = jnp.exp(logits - jnp.max(logits, axis=-1, keepdims=True))
+        rows = pl.ds(pl.multiple_of(block * dec_len, dec_len), dec_len)
+        place = code_ref[rows, :] - base
+        chosen = (place >= 0) & (place < capacity) & (lane_ids < experts)
+        gate_buf[rows, :] = jnp.sum(jnp.where(chosen, powers, 0.0), axis=-1, keepdims=True) / jnp.sum(powers, axis=-1, keepdims=True)
+
+    def absorb_pair(first, second):
+        def body(step, carry):
+            absorb((row + first[0] + step * (second[0] - first[0])) % tp_size, first[1] + step * (second[1] - first[1]), False)
+            return carry
+        lax.fori_loop(0, 2, body, 0)
+
+    absorb(row, 0, True)
+    absorb(row, 1, False)
+    part_copy(below, 0, 0, above).wait_recv()
+    rest_copy(below, 0, above).start()
+    part_copy(above, 1, 1, below).wait_recv()
+    rest_copy(above, 1, below).start()
+    absorb_pair((tp_size - 1, 0), (tp_size + 1, 1))
+    part_copy(below, 1, 0, above).wait_recv()
+    part_copy(above, 0, 1, below).wait_recv()
+    absorb_pair((tp_size - 1, 1), (tp_size + 1, 0))
+    rest_copy(across, 0, above).wait_recv()
+    rest_copy(across, 1, below).wait_recv()
+    absorb_pair((2, 0), (2, 1))
+
     compute_order = (0, 1, chips - 1, 2)
     back_order = (0, chips - 1, 1, 2)
     for relative in compute_order:
         for peer in peers(relative):
             dispatch_copy(peer, me).start()
     recv_buf[me] = send_ref[me]
-    out_ref[...] = states_ref[...]
 
     def compute(relative):
         for peer in peers(relative):
@@ -159,19 +222,20 @@
         near_copy(relative, above, 1, below).wait_recv()
         far_copy(relative, above, 1, below).start()
 
-    def combine(relative):
+    def combine(relative, fresh):
         far_copy(relative, across, 0, above).wait_recv()
         far_copy(relative, across, 1, below).wait_recv()
         which = (chip + relative) % chips
         values = jnp.concatenate([slot_buf[holder, pl.ds(2 * which, 2)].reshape(pair, d_model) for holder in range(tp_size)], axis=0)
-        tile = 256
+        tile = dec_len
 
         def body(step, carry):
+            previous = states_buf[step // own_batch, step % own_batch] if fresh else out_ref[pl.ds(pl.multiple_of(step * tile, tile), tile), :]
             rows = pl.ds(pl.multiple_of(step * tile, tile), tile)
             wanted = code_ref[rows, :] - which * (tp_size * pair)
             pick = (wanted == lax.broadcasted_iota(jnp.int32, (tile, tp_size * pair), 1)).astype(jnp.float32).astype(jnp.bfloat16)
             picked = jnp.dot(pick, values, preferred_element_type=jnp.float32)
-            out_ref[rows, :] = (out_ref[rows, :].astype(jnp.float32) + gate_ref[rows, :] * picked).astype(jnp.bfloat16)
+            out_ref[rows, :] = (previous.astype(jnp.float32) + gate_buf[rows, :] * picked).astype(jnp.bfloat16)
             return carry
 
         lax.fori_loop(0, tokens // tile, body, 0)
@@ -186,14 +250,19 @@
     compute(compute_order[3])
     share(near_2)
     forward(near_1)
-    combine(0)
+    combine(0, True)
     share(near_3)
     forward(near_2)
-    combine(near_1)
+    combine(near_1, False)
     forward(near_3)
-    combine(near_2)
-    combine(near_3)
-
+    combine(near_2, False)
+    combine(near_3, False)
+
+    for part in (0, 1):
+        part_copy(row, part, 0, above).wait_send()
+        part_copy(row, part, 1, below).wait_send()
+    rest_copy(below, 0, above).wait_send()
+    rest_copy(above, 1, below).wait_send()
     for relative in compute_order:
         for peer in peers(relative):
             dispatch_copy(peer, me).wait_send()
@@ -204,31 +273,35 @@
         far_copy(relative, above, 1, below).wait_send()
 
 
-def expert_exchange(send_buf, states, code, gate, w_in, w_out, ep_size, tp_size):
-    capacity, d_model = send_buf.shape[1], send_buf.shape[2]
+def expert_exchange(own, slot_here, code, gain, w_route, w_in, w_out, capacity, experts, ep_size, tp_size):
+    d_model = own.shape[2]
     d_ff = w_in.shape[2]
     vmem = pl.BlockSpec(memory_space=pltpu.VMEM)
     anywhere = pl.BlockSpec(memory_space=pl.ANY)
     dma = pltpu.SemaphoreType.DMA
     chips = ep_size // 2
     return pl.pallas_call(
-        functools.partial(expert_kernel, ep_size, tp_size),
-        out_shape=jax.ShapeDtypeStruct(states.shape, jnp.bfloat16),
-        in_specs=[vmem, vmem, vmem, vmem, anywhere, anywhere],
+        functools.partial(expert_kernel, ep_size, tp_size, capacity, experts),
+        out_shape=jax.ShapeDtypeStruct((code.shape[0], d_model), jnp.bfloat16),
+        in_specs=[vmem, vmem, vmem, vmem, vmem, anywhere, anywhere],
         out_specs=vmem,
         scratch_shapes=[
             pltpu.VMEM((d_model, d_ff), jnp.bfloat16),
             pltpu.VMEM((d_ff, d_model), jnp.bfloat16),
+            pltpu.VMEM((tp_size,) + own.shape, jnp.bfloat16),
+            pltpu.VMEM((code.shape[0], 1), jnp.float32),
+            pltpu.VMEM((ep_size, capacity, d_model), jnp.bfloat16),
             pltpu.VMEM((ep_size, capacity, d_model), jnp.bfloat16),
             pltpu.VMEM((2 * capacity, d_ff), jnp.bfloat16),
             pltpu.VMEM((ep_size, capacity, d_model), jnp.bfloat16),
             pltpu.VMEM((tp_size, ep_size, capacity, d_model), jnp.bfloat16),
-            dma((2,)), dma((ep_size,)), dma((ep_size,)), dma((ep_size,)), dma((ep_size,)),
+            dma((2,)), dma((2, 2)), dma((2, 2)), dma((2,)), dma((2,)),
+            dma((ep_size,)), dma((ep_size,)), dma((ep_size,)), dma((ep_size,)),
             dma((chips, 2)), dma((chips, 2)), dma((chips, 2)), dma((chips, 2)),
         ],
         compiler_params=pltpu.CompilerParams(collective_id=0, has_side_effects=True),
         name='expert_exchange',
-    )(send_buf, states, code, gate, w_in, w_out)
+    )(own, slot_here, code, gain, w_route, w_in, w_out)
 
 
 def solution(mesh):
@@ -280,7 +353,6 @@
         v_own = kv_own[..., width:].reshape(own_batch, -1, tp_size * width)
         context = attention_context(split_heads(queries, all_heads), split_heads(k_own, all_heads), split_heads(v_own, all_heads), pad_bias)
         after_cross = (after_self.astype(jnp.float32) + matmul_f32(context, wo_cross_all)).astype(jnp.bfloat16)
-        after_cross = lax.all_gather(after_cross, 'tp', axis=0, tiled=True)
 
         tokens = batch_dev * dec_len
         experts = w_router.shape[1]
@@ -298,15 +370,9 @@
         code = (owner // 2) * (tp_size * pair_slots) + owner_row * pair_slots + (owner % 2) * capacity + position
         code = jnp.where(kept, code, -1)
 
-        states = after_cross.reshape(tokens, d_model)
-        normed = rms_norm(states, gain_ffn)
-        dispatch = (lax.broadcasted_iota(jnp.int32, (slots, tokens), 0) == slot_here[None, :]).astype(jnp.bfloat16)
-        send_buf = matmul_f32(dispatch, normed).astype(jnp.bfloat16).reshape(ep_size, capacity, d_model)
-
-        logits = sum(matmul_f32(normed, piece) for piece in split_three(w_router))
-        router_prob = jax.nn.softmax(logits, axis=-1)
-        gate_prob = jnp.sum(jnp.where(choice[:, None] == lax.broadcasted_iota(jnp.int32, (tokens, experts), 1), router_prob, 0.0), axis=-1)
-        result = expert_exchange(send_buf, states, code[:, None], gate_prob[:, None], w_in, w_out, ep_size, tp_size)
+        lanes = 128
+        w_route = jnp.concatenate([jnp.pad(piece, ((0, 0), (0, lanes - experts))) for piece in split_three(w_router)], axis=1)
+        result = expert_exchange(after_cross, slot_here.reshape(batch_dev, 1, dec_len), code[:, None], gain_ffn[None], w_route, w_in, w_out, capacity, experts, ep_size, tp_size)
         return result.reshape(batch_dev, dec_len, d_model)
 
     return jax.shard_map(layer, mesh=mesh, in_specs=in_specs, out_specs=token_spec, check_vma=False)

time: 203 us -> 182 us (0.90)
  waiting for transfers between devices: 51.3 us -> 10.4 us
  Pallas kernels: 60.5 us -> 90.2 us
  local copies, waits for them, and re-layouts: 15.3 us -> 11.6 us
  matrix products: 36.8 us -> 33.1 us
  other arithmetic: 13.9 us -> 11.1 us
    all_gather x1 -> x0, waiting for transfers between devices: 31.5 us -> none  [layer(): after_cross = lax.all_gather(after_cross, 'tp', axis=0, tiled=True)]
    pallas_call x1, Pallas kernels: 60.5 us -> 90.2 us  [expert_exchange(): pl.pallas_call(functools.partial(expert_kernel, ep_size, tp_size, capacit...]
    all_gather x1, waiting for transfers between devices: 19.6 us -> 6.14 us  [layer(): w_all = lax.all_gather(w_pack, 'tp', axis=0, tiled=False)]
    dot_general x11 -> x7, matrix products: 19.7 us -> 15.3 us  [matmul_f32(): return jnp.dot(left, right, preferred_element_type=jnp.float32)]
    all_to_all x1, waiting for transfers between devices: 0.01 us -> 4.23 us  [layer(): context = lax.all_to_all(context, 'tp', 0, 2, tiled=True)]
    select_n x1, other arithmetic: 2.14 us -> 0.09 us  [layer(): causal_bias = jnp.where(col_ids <= row_ids, self_bias, NEG_LARGE)[None]]
    unnamed x41 -> x36, local copies, waits for them, and re-layouts: 5.37 us -> 5.36 us
  transfers between devices with their start and end apart: 4 -> 3, of which waited for: 2 -> 2; matrix products, arithmetic and copies ran while one was open for 18% -> 20% of each run, Pallas kernels for 0% -> 0%
where the time goes in v3:
time: 182 us; the launch traced here: 181 us
  Pallas kernels  90.2 us (50%)
  matrix products  33.1 us (18%)
  between operations  13.8 us (8%)
  local copies, waits for them, and re-layouts  11.6 us (6%)
  other arithmetic  11.1 us (6%)
  starting transfers between devices  10.9 us (6%)
  waiting for transfers between devices  10.4 us (6%)
    pallas_call x1, Pallas kernels, expert_exchange(): pl.pallas_call(functools.partial(expert_kernel, ep_size, tp_size, capacit...  90.2 us
    dot_general x7, matrix products, matmul_f32(): return jnp.dot(left, right, preferred_element_type=jnp.float32)  15.3 us
    sub x2, matrix products, attention_context(): weights = jax.nn.softmax(scores, axis=-1).astype(jnp.bfloat16)  9.83 us
    dot_general x2, matrix products, attention_context(): jnp.einsum('bhqk,bkhe->bqhe', weights, values, preferred_element_type=jnp...  6.95 us
    all_to_all x1, starting transfers between devices, layer(): lax.all_to_all(kv_local.reshape(tp_size, own_batch, -1, 2 * width), 'tp',...  6.48 us
    all_gather x1, waiting for transfers between devices, layer(): w_all = lax.all_gather(w_pack, 'tp', axis=0, tiled=False)  6.14 us
    unnamed x36, local copies, waits for them, and re-layouts  5.36 us
    all_to_all x1, starting transfers between devices, layer(): context = lax.all_to_all(context, 'tp', 0, 2, tiled=True)  4.45 us
  transfers between devices with their start and end apart: 3, of which 2 were waited for; matrix products, arithmetic and copies ran while one was open for 20% of the time, Pallas kernels for 0%

profile of v3, /device:TPU:97, one launch (start us, length us, event | category | flops | bytes accessed | tf_op | source)
XLA Modules:
  0.0 181.1 jit_solution(13985927739423298690)
XLA Ops:
  6.5 0.0 copy-start
  6.6 0.0 all-gather.3.cloned.1.call-start
  6.6 2.2 %pad_maximum_fusion = bf16[576,768]{1,0:T(8,128)(2,1)} fusion(bf16[192,768]{1,0:T(8,128)(2,1)} %bitcast.107, bf16[192,768]{1,0:T(8,128)(2,1)} %param.33, bf16[192,768]{1,0:T(8,128)(2,1)} %param.28), kind=kLoop, calls=%fused_computation.76 | loop fusion | flops 2654208 | bytes 1769472 | tf_op jit(solution)/shard_map/concatenate | solution.py:325
  8.8 0.1 all-gather.3.cloned.1.call-update
  8.9 0.0 copy-done
  8.9 1.6 convolution_convert_fusion.2
  10.5 0.0 copy-done.8
  10.5 0.0 copy-start.6
  10.5 0.0 copy-start.5
  10.5 0.7 convolution_convert_fusion.1
  11.2 0.0 copy-start.3
  11.2 0.9 pad_maximum_fusion.1
  12.1 6.5 %all-to-all-start.1 = ((bf16[4,2,128,384]{2,3,1,0:T(8,128)(2,1)}), bf16[4,2,128,384]{2,3,1,0:T(8,128)(2,1)S(1)}, u32[]{:S(2)}, u32[]{:S(2)}) async-start(bf16[4,2,128,384]{2,3,1,0:T(8,128)(2,1)} %pad_maximum_fusion.1), calls=%async_computation.1 | async-start | bytes 1572864 | tf_op jit(solution)/shard_map/all_to_all | solution.py:332
  18.6 0.0 copy-done.6
  18.7 0.0 copy-done.3
  18.7 0.1 broadcast_select_fusion
  18.8 0.2 convolution_bitcast_fusion
  19.0 0.0 copy-done.5
  19.0 0.2 copy.68
  19.2 1.2 copy.49
  20.3 0.1 slice.29
  20.5 0.2 copy.56
  20.7 0.2 copy.57
  20.8 0.3 subtract_reduce_fusion
  21.1 0.1 multiply_reduce_fusion
  21.3 0.2 copy.66
  21.5 2.6 %fusion.2 = f32[8,256]{1,0:T(8,128)S(1)} fusion(bf16[8,256,768]{2,1,0:T(8,128)(2,1)} %param.19), kind=kLoop, calls=%fused_computation.4 | loop fusion | flops 4716544 | bytes 3153920 | tf_op jit(solution)/shard_map/reduce_sum | solution.py:15
  24.1 0.1 fusion.67
  24.2 0.0 copy-done.9
  24.2 0.0 copy-start.2
  24.2 0.0 copy-start.10
  24.2 4.2 %fusion.29 = bf16[8,256,192]{1,2,0:T(8,128)(2,1)} fusion(bf16[8,256,768]{2,1,0:T(8,128)(2,1)} %param.19, f32[768]{0:T(1024)S(1)} %copy-done.12, f32[8,256]{1,0:T(8,128)S(1)} %add_rsqrt_fusion, bf16[768,192]{0,1:T(8,128)(2,1)S(1)} %copy-done.9), kind=kOutput, calls=%fused_computation.44 | convolution fusion | flops 610664448 | bytes 4238336 | tf_op jit(solution)/shard_map/dot_general | solution.py:20
  28.4 0.0 copy-done.2
  28.4 2.2 %fusion.32 = bf16[8,256,192]{1,2,0:T(8,128)(2,1)} fusion(bf16[8,256,768]{2,1,0:T(8,128)(2,1)S(1)} %copy-done.2, f32[768]{0:T(1024)S(1)} %copy-done.12, f32[8,256]{1,0:T(8,128)S(1)} %add_rsqrt_fusion, bf16[768,192]{0,1:T(8,128)(2,1)S(1)} %copy-done.10), kind=kOutput, calls=%fused_computation.45 | convolution fusion | flops 610664448 | bytes 4238336 | tf_op jit(solution)/shard_map/dot_general | solution.py:20
  30.6 0.0 copy-done.11
  30.6 2.2 %fusion.26 = bf16[8,256,192]{1,2,0:T(8,128)(2,1)} fusion(bf16[8,256,768]{2,1,0:T(8,128)(2,1)S(1)} %copy-done.2, f32[768]{0:T(1024)S(1)} %copy-done.12, f32[8,256]{1,0:T(8,128)S(1)} %add_rsqrt_fusion, bf16[768,192]{0,1:T(8,128)(2,1)S(1)} %copy-done.11), kind=kOutput, calls=%fused_computation.43 | convolution fusion | flops 610664448 | bytes 4238336 | tf_op jit(solution)/shard_map/dot_general | solution.py:20
  32.8 6.1 %fusion.83 = (f32[8,3,256]{2,1,0:T(4,128)S(1)}, f32[8,3,256,256]{2,3,1,0:T(8,128)}) fusion(f32[3,256,256]{1,2,0:T(8,128)S(1)} %copy-done.4, bf16[8,256,3,64]{1,3,2,0:T(8,128)(2,1)} %bitcast.112, bf16[8,256,3,64]{1,3,2,0:T(8,128)(2,1)} %bitcast.113), kind=kOutput, calls=%fused_computation.120 | convolution fusion | flops 206045440 | bytes 8675328 | tf_op jit(solution)/shard_map/sub | solution.py:29
  38.9 4.6 %fusion.36 = bf16[8,3,64,256]{3,2,1,0:T(8,128)(2,1)} fusion(bf16[8,256,3,64]{1,3,2,0:T(8,128)(2,1)} %bitcast.111, f32[8,3,256,256]{2,3,1,0:T(8,128)} %get-tuple-element.12, f32[8,3,256]{2,1,0:T(4,128)S(1)} %get-tuple-element.11), kind=kOutput, calls=%fused_computation.48 | convolution fusion | flops 204865536 | bytes 7888896 | tf_op jit(solution)/shard_map/bhqk,bkhe->bqhe/dot_general | solution.py:30
  43.5 0.9 fusion.59.route_ref
  44.5 0.4 copy.58
  44.8 0.0 copy-start.7
  44.9 0.4 copy.74
  45.2 3.0 %fusion.45.code_ref = s32[2048,1]{1,0:T(8,128)} fusion(s32[2048,1]{1,0:T(8,128)S(1)} %copy.58, s32[1,2048]{0,1:T(8,128)S(1)} %copy.74), kind=kLoop, calls=%fused_computation.63 | loop fusion | flops 94208 | bytes 24576 | tf_op jit(solution)/shard_map/jit(_where)/select_n | solution.py:371
  48.2 0.0 all-to-all-done.1
  48.2 4.5 %all-to-all-start = ((bf16[8,256,192]{1,2,0:T(8,128)(2,1)}), bf16[8,256,192]{1,2,0:T(8,128)(2,1)}, u32[]{:S(2)}, u32[]{:S(2)}) async-start(bf16[8,256,192]{1,2,0:T(8,128)(2,1)} %bitcast.101), calls=%async_computation | async-start | bytes 1572864 | tf_op jit(solution)/shard_map/all_to_all | solution.py:342
  52.7 0.7 compare_select_fusion
  53.4 0.6 select_n.91.slot_ref
  54.0 0.6 broadcast_in_dim.38.gain_ref
  54.6 0.1 fusion.82
  54.6 0.8 copy.53
  55.5 6.1 %all-gather.3.cloned.1.call-done = bf16[2304,768]{1,0:T(8,128)(2,1)} async-done(((bf16[576,768]{1,0:T(8,128)(2,1)}), bf16[2304,768]{1,0:T(8,128)(2,1)}) %all-gather.3.cloned.1.call-update) | async-done | bytes 3538960 | tf_op jit(solution)/shard_map/all_gather | solution.py:326
  61.6 1.8 fusion.81
  63.4 4.2 %all-to-all-done = bf16[8,256,192]{1,2,0:T(8,128)(2,1)} async-done(((bf16[8,256,192]{1,2,0:T(8,128)(2,1)}), bf16[8,256,192]{1,2,0:T(8,128)(2,1)}, u32[]{:S(2)}, u32[]{:S(2)}) %all-to-all-start) | async-done | bytes 786464 | tf_op jit(solution)/shard_map/all_to_all | solution.py:342
  67.6 2.7 %fusion.19 = (f32[2,256]{1,0:T(2,128)S(1)}, bf16[2,256,768]{2,1,0:T(8,128)(2,1)S(1)}) fusion(bf16[2,256,4,192]{1,3,0,2:T(8,128)(2,1)} %bitcast.9, bf16[4,576,768]{2,1,0:T(8,128)(2,1)} %bitcast.98, bf16[8,256,768]{2,1,0:T(8,128)(2,1)} %param.19, s32[]{:T(128)S(6)} %select_n.85), kind=kOutput, calls=%fused_computation.25 | convolution fusion | flops 606338560 | bytes 3540996 | tf_op jit(solution)/shard_map/dot_general | solution.py:20
  70.3 0.9 copy-done.14
  71.2 0.0 copy-done.13
  71.2 0.8 convolution_convert_fusion
  72.0 0.3 copy.52
  72.3 3.8 %fusion.84 = (f32[2,12,256]{2,1,0:T(8,128)S(1)}, f32[2,12,256,128]{2,3,1,0:T(8,128)}) fusion(f32[2,128]{1,0:T(2,128)S(1)} %compare_select_fusion, bf16[2,256,12,64]{1,3,2,0:T(8,128)(2,1)S(1)} %bitcast.102, bf16[2,128,12,64]{1,3,2,0:T(8,128)(2,1)} %bitcast.104), kind=kOutput, calls=%fused_computation.121 | convolution fusion | flops 103022720 | bytes 4350976 | tf_op jit(solution)/shard_map/sub | solution.py:29
  76.1 2.3 %fusion.35 = bf16[2,12,64,256]{3,2,1,0:T(8,128)(2,1)S(1)} fusion(bf16[2,128,12,64]{1,3,2,0:T(8,128)(2,1)S(1)} %bitcast.103, f32[2,12,256,128]{2,3,1,0:T(8,128)} %get-tuple-element.16, f32[2,12,256]{2,1,0:T(8,128)S(1)} %get-tuple-element.15), kind=kOutput, calls=%fused_computation.47 | convolution fusion | flops 102629376 | bytes 4349952 | tf_op jit(solution)/shard_map/bhqk,bkhe->bqhe/dot_general | solution.py:30
  78.4 1.7 fusion.22.own_ref
  80.2 90.2 %expert_exchange.1 = bf16[2048,768]{1,0:T(8,128)(2,1)} custom-call(bf16[2,256,768]{2,1,0:T(8,128)(2,1)} %fusion.22.own_ref, s32[8,1,256]{2,1,0:T(1,128)} %select_n.91.slot_ref, s32[2048,1]{1,0:T(8,128)} %fusion.45.code_ref, f32[1,768]{1,0:T(1,128)} %broadcast_in_dim.38.gain_ref, bf16[768,384]{1,0:T(8,128)(2,1)} %fusion.59.route_ref, ...), custom_call_target="tpu_custom_call" | custom-call | tf_op jit(solution)/shard_map/expert_exchange/pallas_call | solution.py:283
  170.4 0.0 copy-start.1
  170.4 3.9 %copy.76 = bf16[8,256,768]{2,1,0:T(8,128)(2,1)} copy(bf16[8,256,768]{2,1,0:T(8,128)(2,1)} %bitcast.95) | data formatting | bytes 6291456
  (25 shorter events, 0.2 us)
Async XLA Ops:
  6.5 2.3 %copy-start = (bf16[8,128,768]{2,1,0:T(8,128)(2,1)S(1)}, bf16[8,128,768]{2,1,0:T(8,128)(2,1)}, u32[]{:S(2)}) copy-start(bf16[8,128,768]{2,1,0:T(8,128)(2,1)} %param.20) | copy-start | bytes 4718596
  6.6 4.0 %copy-start.8 = (bf16[768,192]{0,1:T(8,128)(2,1)S(1)}, bf16[768,192]{0,1:T(8,128)(2,1)}, u32[]{:S(2)}) copy-start(bf16[768,192]{0,1:T(8,128)(2,1)} %param.32) | copy-start | bytes 884740
  6.6 55.1 %all-gather.3.cloned.1.call-start = ((), (), s32[]{:S(2)}) async-start(), calls=%async_computation.2 | async-start | bytes 4423680 | tf_op jit(solution)/shard_map/all_gather | solution.py:326
  10.5 8.1 %copy-start.6 = (s32[8,256]{1,0:T(8,128)S(1)}, s32[8,256]{1,0:T(8,128)}, u32[]{:S(2)}) copy-start(s32[8,256]{1,0:T(8,128)} %param.22) | copy-start | bytes 24580
  10.5 8.5 %copy-start.5 = (f32[768,32]{0,1:T(8,128)S(1)}, f32[768,32]{0,1:T(8,128)}, u32[]{:S(2)}) copy-start(f32[768,32]{0,1:T(8,128)} %param.35) | copy-start | bytes 294916
  11.2 7.5 %copy-start.3 = (f32[3,256,256]{2,1,0:T(8,128)S(1)}, f32[3,256,256]{2,1,0:T(8,128)}, u32[]{:S(2)}) copy-start(f32[3,256,256]{2,1,0:T(8,128)} %param.23) | copy-start | bytes 2359300
  12.1 36.1 %all-to-all-start.1 = ((bf16[4,2,128,384]{2,3,1,0:T(8,128)(2,1)}), bf16[4,2,128,384]{2,3,1,0:T(8,128)(2,1)S(1)}, u32[]{:S(2)}, u32[]{:S(2)}) async-start(bf16[4,2,128,384]{2,3,1,0:T(8,128)(2,1)} %pad_maximum_fusion.1), calls=%async_computation.1 | async-start | bytes 1572864 | tf_op jit(solution)/shard_map/all_to_all | solution.py:332
  20.3 3.8 %copy-start.9 = (bf16[768,192]{0,1:T(8,128)(2,1)S(1)}, bf16[768,192]{0,1:T(8,128)(2,1)}, u32[]{:S(2)}) copy-start(bf16[768,192]{0,1:T(8,128)(2,1)} %param.25) | copy-start | bytes 884740
  20.3 3.8 %copy-start.12 = (f32[768]{0:T(1024)S(1)}, f32[768]{0:T(1024)}, u32[]{:S(2)}) copy-start(f32[768]{0:T(1024)} %param.24) | copy-start | bytes 9220
  24.2 4.2 %copy-start.2 = (bf16[8,256,768]{2,1,0:T(8,128)(2,1)S(1)}, bf16[8,256,768]{2,1,0:T(8,128)(2,1)}, u32[]{:S(2)}) copy-start(bf16[8,256,768]{2,1,0:T(8,128)(2,1)} %param.19) | copy-start | bytes 9437188
  24.2 4.2 %copy-start.10 = (bf16[768,192]{0,1:T(8,128)(2,1)S(1)}, bf16[768,192]{0,1:T(8,128)(2,1)}, u32[]{:S(2)}) copy-start(bf16[768,192]{0,1:T(8,128)(2,1)} %param.26) | copy-start | bytes 884740
  28.4 2.2 %copy-start.11 = (bf16[768,192]{0,1:T(8,128)(2,1)S(1)}, bf16[768,192]{0,1:T(8,128)(2,1)}, u32[]{:S(2)}) copy-start(bf16[768,192]{0,1:T(8,128)(2,1)} %param.27) | copy-start | bytes 884740
  30.6 2.2 %copy-start.4 = (f32[3,256,256]{1,2,0:T(8,128)S(1)}, f32[3,256,256]{1,2,0:T(8,128)}, u32[]{:S(2)}) copy-start(f32[3,256,256]{1,2,0:T(8,128)} %copy.49) | copy-start | bytes 2359300
  44.8 9.2 %copy-start.7 = (f32[768]{0:T(1024)S(1)}, f32[768]{0:T(1024)}, u32[]{:S(2)}) copy-start(f32[768]{0:T(1024)} %param.34) | copy-start | bytes 9220
  48.2 19.4 %all-to-all-start = ((bf16[8,256,192]{1,2,0:T(8,128)(2,1)}), bf16[8,256,192]{1,2,0:T(8,128)(2,1)}, u32[]{:S(2)}, u32[]{:S(2)}) async-start(bf16[8,256,192]{1,2,0:T(8,128)(2,1)} %bitcast.101), calls=%async_computation | async-start | bytes 1572864 | tf_op jit(solution)/shard_map/all_to_all | solution.py:342
  67.6 3.6 %copy-start.13 = (f32[768]{0:T(1024)S(1)}, f32[768]{0:T(1024)}, u32[]{:S(2)}) copy-start(f32[768]{0:T(1024)} %param.29) | copy-start | bytes 9220
  70.3 0.9 copy-start.14
  76.1 2.3 %copy-start.15 = (bf16[2,256,768]{2,1,0:T(8,128)(2,1)S(1)}, bf16[2,256,768]{2,1,0:T(8,128)(2,1)}, u32[]{:S(2)}) copy-start(bf16[2,256,768]{2,1,0:T(8,128)(2,1)} %copy-done.14) | copy-start | bytes 2359300
  170.4 3.9 %copy-start.1 = (bf16[8,128,768]{2,1,0:T(8,128)(2,1)S(1)}, bf16[8,128,768]{2,1,0:T(8,128)(2,1)}, u32[]{:S(2)}) copy-start(bf16[8,128,768]{2,1,0:T(8,128)(2,1)} %param.20) | copy-start | bytes 4718596
Sparse Core Ops, SparseCore 0:
  9.0 52.5 all-gather.2

commit v4 on v3

--- a/solution.py
+++ b/solution.py
@@ -8,27 +8,6 @@
 
 EPSILON = 1e-6
 NEG_LARGE = -1e30
-
-
-def rms_norm(states, gain_vec):
-    upcast = states.astype(jnp.float32)
-    mean_sq = jnp.mean(upcast * upcast, axis=-1, keepdims=True)
-    return (upcast * lax.rsqrt(mean_sq + EPSILON) * gain_vec).astype(jnp.bfloat16)
-
-
-def matmul_f32(left, right):
-    return jnp.dot(left, right, preferred_element_type=jnp.float32)
-
-
-def split_heads(flat, heads):
-    return flat.reshape(flat.shape[0], flat.shape[1], heads, flat.shape[2] // heads)
-
-
-def attention_context(queries, key_heads, values, bias_mask):
-    scores = jnp.einsum('bqhe,bkhe->bhqk', queries, key_heads, preferred_element_type=jnp.float32) + bias_mask
-    weights = jax.nn.softmax(scores, axis=-1).astype(jnp.bfloat16)
-    context = jnp.einsum('bhqk,bkhe->bqhe', weights, values, preferred_element_type=jnp.float32).astype(jnp.bfloat16)
-    return context.reshape(context.shape[0], context.shape[1], -1)
 
 
 def split_three(weight):
@@ -304,6 +283,271 @@
     )(own, slot_here, code, gain, w_route, w_in, w_out)
 
 
+def attend(queries, key_heads, values, allowed, bias):
+    scores = lax.dot_general(queries, key_heads, (((1,), (1,)), ((), ())), preferred_element_type=jnp.float32)
+    if bias is not None:
+        scores = scores + bias
+    scores = jnp.where(allowed, scores, NEG_LARGE)
+    powers = jnp.exp(scores - jnp.max(scores, axis=-1, keepdims=True))
+    weights = (powers / jnp.sum(powers, axis=-1, keepdims=True)).astype(jnp.bfloat16)
+    return jnp.dot(weights, values, preferred_element_type=jnp.float32).astype(jnp.bfloat16)
+
+
+def attention_kernel(tp_size, heads, dec_ref, enc_ref, pad_ref, bias_ref, gain_self_ref, gain_cross_ref, wq_ref, wk_ref, wv_ref, wo_ref, wq_cross_ref, wk_cross_ref, wv_cross_ref, wo_cross_ref, out_ref, dec_buf, enc_buf, weight_buf, kv_send, kv_recv, kv_relay, ctx_send, ctx_recv, ctx_relay, mixed_buf, dec_sem, enc_sem, wn_send, wn_recv, wf_send, wf_recv, wp_send, wp_recv, kv_sems, ctx_sems):
+    me = lax.axis_index('ep')
+    row = lax.axis_index('tp')
+    core = me % 2
+    partner = me + 1 - 2 * core
+    above = (row + 1) % tp_size
+    below = (row + tp_size - 1) % tp_size
+    across = (row + 2) % tp_size
+    width = wo_ref.shape[0]
+    head = width // heads
+    batch_dev, dec_len, d_model = dec_ref.shape
+    enc_len = enc_ref.shape[1]
+
+    enc_copy = pltpu.make_async_copy(enc_ref, enc_buf, enc_sem.at[0])
+    enc_copy.start()
+
+    def dec_copy(block):
+        return pltpu.make_async_copy(dec_ref.at[pl.ds(2 * block, 2)], dec_buf.at[pl.ds(2 * block, 2)], dec_sem.at[block])
+
+    for block in range(tp_size):
+        dec_copy(block).start()
+
+    barrier = pltpu.get_barrier_semaphore()
+    pl.semaphore_signal(barrier, inc=1, device_id={'ep': partner}, device_id_type=MESH_ID)
+    for neighbour in (above, below):
+        pl.semaphore_signal(barrier, inc=1, device_id={'tp': neighbour}, device_id_type=MESH_ID)
+
+    weight_buf[row, 0:width] = wo_ref[...]
+    weight_buf[row, width:2 * width] = wq_cross_ref[...].astype(jnp.float32).T.astype(jnp.bfloat16)
+    weight_buf[row, 2 * width:3 * width] = wo_cross_ref[...]
+    pl.semaphore_wait(barrier, 3)
+
+    groups = ((0, 2 * width), (2 * width, width))
+
+    def near_weights(group, holder, side, target):
+        start, size = groups[group]
+        rows = pl.ds(pl.multiple_of(start + core * (size // 2), 32), size // 2)
+        return pltpu.make_async_remote_copy(
+            src_ref=weight_buf.at[holder, rows], dst_ref=weight_buf.at[holder, rows],
+            send_sem=wn_send.at[group, side], recv_sem=wn_recv.at[group, side],
+            device_id={'tp': target}, device_id_type=MESH_ID)
+
+    def far_weights(group, holder, side, target):
+        start, size = groups[group]
+        rows = pl.ds(pl.multiple_of(start + core * (size // 2) + side * (size // 4), 16), size // 4)
+        return pltpu.make_async_remote_copy(
+            src_ref=weight_buf.at[holder, rows], dst_ref=weight_buf.at[holder, rows],
+            send_sem=wf_send.at[group, side], recv_sem=wf_recv.at[group, side],
+            device_id={'tp': target}, device_id_type=MESH_ID)
+
+    def pass_weights(group, holder, which, half):
+        start, size = groups[group]
+        rows = pl.ds(pl.multiple_of(start + half * (size // 2), 32), size // 2)
+        return pltpu.make_async_remote_copy(
+            src_ref=weight_buf.at[holder, rows], dst_ref=weight_buf.at[holder, rows],
+            send_sem=wp_send.at[group, which], recv_sem=wp_recv.at[group, which],
+            device_id={'ep': partner}, device_id_type=MESH_ID)
+
+    def exchange(sent, received, relay, sems):
+        half = dec_len // 2
+
+        def near(block, source, side, target):
+            return pltpu.make_async_remote_copy(
+                src_ref=sent.at[block], dst_ref=received.at[source], send_sem=sems.at[0, side], recv_sem=sems.at[1, side],
+                device_id={'tp': target}, device_id_type=MESH_ID)
+
+        def first_hop(side, target):
+            return pltpu.make_async_remote_copy(
+                src_ref=sent.at[across, pl.ds(side * half, half)], dst_ref=relay.at[side], send_sem=sems.at[2, side], recv_sem=sems.at[3, side],
+                device_id={'tp': target}, device_id_type=MESH_ID)
+
+        def second_hop(source, side, target):
+            return pltpu.make_async_remote_copy(
+                src_ref=relay.at[side], dst_ref=received.at[source, pl.ds(side * half, half)], send_sem=sems.at[4, side], recv_sem=sems.at[5, side],
+                device_id={'tp': target}, device_id_type=MESH_ID)
+
+        def start():
+            first_hop(0, above).start()
+            first_hop(1, below).start()
+            near(above, row, 0, above).start()
+            near(below, row, 1, below).start()
+
+        def relay_on():
+            first_hop(0, above).wait_recv()
+            second_hop(below, 0, above).start()
+            first_hop(1, below).wait_recv()
+            second_hop(above, 1, below).start()
+
+        def finish():
+            near(above, below, 0, above).wait_recv()
+            near(below, above, 1, below).wait_recv()
+            second_hop(across, 0, above).wait_recv()
+            second_hop(across, 1, below).wait_recv()
+
+        def drain():
+            first_hop(0, above).wait_send()
+            first_hop(1, below).wait_send()
+            near(above, row, 0, above).wait_send()
+            near(below, row, 1, below).wait_send()
+            second_hop(below, 0, above).wait_send()
+            second_hop(above, 1, below).wait_send()
+
+        return start, relay_on, finish, drain
+
+    kv_start, kv_relay_on, kv_finish, kv_drain = exchange(kv_send, kv_recv, kv_relay, kv_sems)
+    ctx_start, ctx_relay_on, ctx_finish, ctx_drain = exchange(ctx_send, ctx_recv, ctx_relay, ctx_sems)
+
+    near_weights(0, row, 0, above).start()
+    near_weights(0, row, 1, below).start()
+
+    enc_copy.wait()
+
+    def project_kv(block, carry):
+        source = enc_buf[pl.ds(2 * block, 2)].reshape(2 * enc_len, d_model)
+        keys = jnp.dot(source, wk_cross_ref[...], preferred_element_type=jnp.float32).astype(jnp.bfloat16)
+        values = jnp.dot(source, wv_cross_ref[...], preferred_element_type=jnp.float32).astype(jnp.bfloat16)
+        kv_send[block] = jnp.concatenate([keys, values], axis=-1)
+        return carry
+
+    lax.fori_loop(0, tp_size, project_kv, 0)
+    kv_start()
+
+    causal = lax.broadcasted_iota(jnp.int32, (dec_len, dec_len), 1) <= lax.broadcasted_iota(jnp.int32, (dec_len, dec_len), 0)
+
+    def normalise(upcast, gain):
+        mean_sq = jnp.mean(upcast * upcast, axis=-1, keepdims=True)
+        return (upcast * lax.rsqrt(mean_sq + EPSILON) * gain).astype(jnp.bfloat16)
+
+    def self_block(block, carry):
+        dec_copy(block).wait()
+        normed = normalise(dec_buf[pl.ds(2 * block, 2)].reshape(2 * dec_len, d_model).astype(jnp.float32), gain_self_ref[...])
+        queries = jnp.dot(normed, wq_ref[...], preferred_element_type=jnp.float32).astype(jnp.bfloat16)
+        keys = jnp.dot(normed, wk_ref[...], preferred_element_type=jnp.float32).astype(jnp.bfloat16)
+        values = jnp.dot(normed, wv_ref[...], preferred_element_type=jnp.float32).astype(jnp.bfloat16)
+        pieces = []
+        for seq in range(2):
+            rows = slice(seq * dec_len, (seq + 1) * dec_len)
+            for which in range(heads):
+                lanes = slice(which * head, (which + 1) * head)
+                pieces.append(attend(queries[rows, lanes], keys[rows, lanes], values[rows, lanes], causal, bias_ref[which]))
+        ctx_send[block] = jnp.concatenate(pieces, axis=-1)
+        return carry
+
+    lax.fori_loop(0, tp_size, self_block, 0)
+    ctx_start()
+    ctx_recv[row] = ctx_send[row]
+    kv_recv[row] = kv_send[row]
+
+    def weights_forward(group):
+        near_weights(group, below, 0, above).wait_recv()
+        far_weights(group, below, 0, above).start()
+        pass_weights(group, below, 0, core).start()
+        near_weights(group, above, 1, below).wait_recv()
+        far_weights(group, above, 1, below).start()
+        pass_weights(group, above, 1, core).start()
+
+    def weights_pass_far(group):
+        far_weights(group, across, 0, above).wait_recv()
+        far_weights(group, across, 1, below).wait_recv()
+        pass_weights(group, across, 2, core).start()
+
+    def weights_finish(group):
+        pass_weights(group, below, 0, 1 - core).wait_recv()
+        pass_weights(group, above, 1, 1 - core).wait_recv()
+        pass_weights(group, across, 2, 1 - core).wait_recv()
+
+    weights_forward(0)
+    kv_relay_on()
+    near_weights(1, row, 0, above).start()
+    near_weights(1, row, 1, below).start()
+    weights_pass_far(0)
+    weights_finish(0)
+    ctx_relay_on()
+    ctx_finish()
+
+    for seq in range(2):
+        update = None
+        for source in range(tp_size):
+            context = ctx_recv[source, :, seq * width:(seq + 1) * width]
+            term = jnp.dot(context, weight_buf[source, 0:width], preferred_element_type=jnp.float32)
+            update = term if update is None else update + term
+        out_ref[seq] = (dec_buf[2 * row + seq].astype(jnp.float32) + update).astype(jnp.bfloat16)
+    weights_forward(1)
+    kv_finish()
+    normed = normalise(out_ref[...].reshape(2 * dec_len, d_model).astype(jnp.float32), gain_cross_ref[...])
+
+    def cross_block(source, carry):
+        queries = lax.dot_general(normed, weight_buf[source, width:2 * width], (((1,), (1,)), ((), ())), preferred_element_type=jnp.float32).astype(jnp.bfloat16)
+        key_values = kv_recv[source]
+        for seq in range(2):
+            allowed = pad_ref[pl.ds(2 * row + seq, 1), :] == 0
+            rows = slice(seq * dec_len, (seq + 1) * dec_len)
+            key_rows = slice(seq * enc_len, (seq + 1) * enc_len)
+            pieces = []
+            for which in range(heads):
+                lanes = slice(which * head, (which + 1) * head)
+                value_lanes = slice(width + which * head, width + (which + 1) * head)
+                pieces.append(attend(queries[rows, lanes], key_values[key_rows, lanes], key_values[key_rows, value_lanes], allowed, None))
+            mixed_buf[source, rows] = jnp.concatenate(pieces, axis=-1)
+        return carry
+
+    lax.fori_loop(0, tp_size, cross_block, 0)
+    weights_pass_far(1)
+    weights_finish(1)
+    for seq in range(2):
+        update = None
+        for source in range(tp_size):
+            context = mixed_buf[source, seq * dec_len:(seq + 1) * dec_len]
+            term = jnp.dot(context, weight_buf[source, 2 * width:3 * width], preferred_element_type=jnp.float32)
+            update = term if update is None else update + term
+        out_ref[seq] = (out_ref[seq].astype(jnp.float32) + update).astype(jnp.bfloat16)
+
+    kv_drain()
+    ctx_drain()
+    for group in range(2):
+        near_weights(group, row, 0, above).wait_send()
+        near_weights(group, row, 1, below).wait_send()
+        far_weights(group, below, 0, above).wait_send()
+        far_weights(group, above, 1, below).wait_send()
+        pass_weights(group, below, 0, core).wait_send()
+        pass_weights(group, above, 1, core).wait_send()
+        pass_weights(group, across, 2, core).wait_send()
+
+
+def attention_front(arrays, heads, tp_size):
+    dec_states, enc_states, wo_self = arrays[0], arrays[1], arrays[9]
+    batch_dev, dec_len, d_model = dec_states.shape
+    enc_len = enc_states.shape[1]
+    width = wo_self.shape[0]
+    vmem = pl.BlockSpec(memory_space=pltpu.VMEM)
+    anywhere = pl.BlockSpec(memory_space=pl.ANY)
+    dma = pltpu.SemaphoreType.DMA
+    block = (tp_size, dec_len, 2 * width)
+    relay = (2, dec_len // 2, 2 * width)
+    return pl.pallas_call(
+        functools.partial(attention_kernel, tp_size, heads),
+        out_shape=jax.ShapeDtypeStruct((batch_dev // tp_size, dec_len, d_model), jnp.bfloat16),
+        in_specs=[anywhere, anywhere] + [vmem] * (len(arrays) - 2),
+        out_specs=vmem,
+        scratch_shapes=[
+            pltpu.VMEM(dec_states.shape, jnp.bfloat16),
+            pltpu.VMEM(enc_states.shape, jnp.bfloat16),
+            pltpu.VMEM((tp_size, 3 * width, d_model), jnp.bfloat16),
+            pltpu.VMEM(block, jnp.bfloat16), pltpu.VMEM(block, jnp.bfloat16), pltpu.VMEM(relay, jnp.bfloat16),
+            pltpu.VMEM(block, jnp.bfloat16), pltpu.VMEM(block, jnp.bfloat16), pltpu.VMEM(relay, jnp.bfloat16),
+            pltpu.VMEM((tp_size, 2 * dec_len, width), jnp.bfloat16),
+            dma((tp_size,)), dma((1,)),
+            dma((2, 2)), dma((2, 2)), dma((2, 2)), dma((2, 2)), dma((2, 3)), dma((2, 3)),
+            dma((6, 2)), dma((6, 2)),
+        ],
+        compiler_params=pltpu.CompilerParams(collective_id=1, has_side_effects=True),
+        name='attention_front',
+    )(*arrays)
+
+
 def solution(mesh):
     ep_size = mesh.shape['ep']
     tp_size = mesh.shape['tp']
@@ -318,41 +562,8 @@
     def layer(dec_states, enc_states, enc_pad, expert_idx, self_bias, gain_self, wq_self, wk_self, wv_self, wo_self, gain_cross, wq_cross, wk_cross, wv_cross, wo_cross, gain_ffn, w_router, w_in, w_out):
         batch_dev, dec_len, d_model = dec_states.shape
         heads = self_bias.shape[0]
-        width = wo_self.shape[0]
-        own_batch = batch_dev // tp_size
         tp_id = lax.axis_index('tp')
-
-        w_pack = jnp.concatenate([wo_self, wo_cross, wq_cross.T], axis=0)
-        w_all = lax.all_gather(w_pack, 'tp', axis=0, tiled=False)
-        wo_self_all = w_all[:, :width].reshape(tp_size * width, d_model)
-        wo_cross_all = w_all[:, width:2 * width].reshape(tp_size * width, d_model)
-        wq_cross_all = w_all[:, 2 * width:].reshape(tp_size * width, d_model)
-
-        kv_local = jnp.concatenate([matmul_f32(enc_states, wk_cross), matmul_f32(enc_states, wv_cross)], axis=-1).astype(jnp.bfloat16)
-        kv_own = lax.all_to_all(kv_local.reshape(tp_size, own_batch, -1, 2 * width), 'tp', 0, 0, tiled=True)
-
-        row_ids = lax.broadcasted_iota(jnp.int32, (dec_len, dec_len), 0)
-        col_ids = lax.broadcasted_iota(jnp.int32, (dec_len, dec_len), 1)
-        causal_bias = jnp.where(col_ids <= row_ids, self_bias, NEG_LARGE)[None]
-        normed = rms_norm(dec_states, gain_self)
-        queries = split_heads(matmul_f32(normed, wq_self).astype(jnp.bfloat16), heads)
-        key_heads = split_heads(matmul_f32(normed, wk_self).astype(jnp.bfloat16), heads)
-        values = split_heads(matmul_f32(normed, wv_self).astype(jnp.bfloat16), heads)
-        context = attention_context(queries, key_heads, values, causal_bias)
-        context = lax.all_to_all(context, 'tp', 0, 2, tiled=True)
-        dec_own = lax.dynamic_slice_in_dim(dec_states, tp_id * own_batch, own_batch, 0)
-        after_self = (dec_own.astype(jnp.float32) + matmul_f32(context, wo_self_all)).astype(jnp.bfloat16)
-
-        pad_own = lax.dynamic_slice_in_dim(enc_pad, tp_id * own_batch, own_batch, 0)
-        pad_bias = jnp.where(pad_own == 0, 0.0, NEG_LARGE).astype(jnp.float32)[:, None, None, :]
-        normed = rms_norm(after_self, gain_cross)
-        all_heads = heads * tp_size
-        queries = jnp.einsum('bld,kd->blk', normed, wq_cross_all, preferred_element_type=jnp.float32).astype(jnp.bfloat16)
-        kv_own = jnp.transpose(kv_own, (1, 2, 0, 3))
-        k_own = kv_own[..., :width].reshape(own_batch, -1, tp_size * width)
-        v_own = kv_own[..., width:].reshape(own_batch, -1, tp_size * width)
-        context = attention_context(split_heads(queries, all_heads), split_heads(k_own, all_heads), split_heads(v_own, all_heads), pad_bias)
-        after_cross = (after_self.astype(jnp.float32) + matmul_f32(context, wo_cross_all)).astype(jnp.bfloat16)
+        after_cross = attention_front([dec_states, enc_states, enc_pad, self_bias, gain_self[None], gain_cross[None], wq_self, wk_self, wv_self, wo_self, wq_cross, wk_cross, wv_cross, wo_cross], heads, tp_size)
 
         tokens = batch_dev * dec_len
         experts = w_router.shape[1]

time: 182 us -> 167 us (0.918)
  Pallas kernels: 90.2 us -> 144 us
  matrix products: 33.1 us -> 0.19 us
  between operations: 13.8 us -> 0.17 us
  starting transfers between devices: 10.9 us -> 0 us
  waiting for transfers between devices: 10.4 us -> 0 us
  other arithmetic: 11.1 us -> 5.36 us
  local copies, waits for them, and re-layouts: 11.6 us -> 16.7 us
    pallas_call x0 -> x1, Pallas kernels: none -> 54.7 us  [attention_front(): pl.pallas_call(functools.partial(attention_kernel, tp_size, heads), out_s...]
    dot_general x10 -> x0, matrix products: 23.1 us -> none  [the longest x7 15.3 us: matmul_f32(): return jnp.dot(left, right, preferred_element_type=jnp.float32)]
    all_to_all x2 -> x0, starting transfers between devices: 10.9 us -> none  [the longest x1 6.48 us: layer(): lax.all_to_all(kv_local.reshape(tp_size, own_batch, -1, 2 * width), 'tp',...]
    sub x2 -> x0, matrix products: 9.83 us -> none  [attention_context(): weights = jax.nn.softmax(scores, axis=-1).astype(jnp.bfloat16)]
    all_gather x1 -> x0, waiting for transfers between devices: 6.14 us -> none  [layer(): w_all = lax.all_gather(w_pack, 'tp', axis=0, tiled=False)]
    unnamed x36 -> x26, local copies, waits for them, and re-layouts: 5.36 us -> 10.5 us
    all_to_all x2 -> x0, waiting for transfers between devices: 4.23 us -> none  [the longest x1 4.23 us: layer(): context = lax.all_to_all(context, 'tp', 0, 2, tiled=True)]
    concatenate x2 -> x0, other arithmetic: 3.17 us -> none  [the longest x1 2.24 us: layer(): w_pack = jnp.concatenate([wo_self, wo_cross, wq_cross.T], axis=0)]
  transfers between devices with their start and end apart: 3 -> 0, of which waited for: 2 -> 0; matrix products, arithmetic and copies ran while one was open for 20% -> 0% of each run, Pallas kernels for 0% -> 0%
where the time goes in v4:
time: 167 us
  Pallas kernels  144 us (86%)
  local copies, waits for them, and re-layouts  16.7 us (10%)
  other arithmetic  5.36 us (3%)
    pallas_call x1, Pallas kernels, expert_exchange(): pl.pallas_call(functools.partial(expert_kernel, ep_size, tp_size, capacit...  89.7 us
    pallas_call x1, Pallas kernels, attention_front(): pl.pallas_call(functools.partial(attention_kernel, tp_size, heads), out_s...  54.7 us
    unnamed x26, local copies, waits for them, and re-layouts  10.5 us

profile of v4, /device:TPU:97, one launch (start us, length us, event | category | flops | bytes accessed | tf_op | source)
XLA Modules:
  0.0 166.7 jit_solution(42181076822748334)
XLA Ops:
  0.0 1.3 broadcast_in_dim.14.gain_self_ref
  1.3 1.3 broadcast_in_dim.15.gain_cross_ref
  2.6 1.3 broadcast_in_dim.16.gain_ref
  3.8 0.7 eq.23
  4.5 0.7 copy.65
  5.2 0.9 convert_element_type.51
  6.1 0.0 copy-start.7
  6.2 0.2 copy.62
  6.3 0.0 copy-start.1
  6.3 0.2 convolution_bitcast_fusion
  6.5 0.1 slice.4
  6.7 0.0 copy-start.2
  6.7 0.2 copy.52
  6.9 0.2 copy.53
  7.0 0.0 copy-start.3
  7.0 0.3 subtract_reduce_fusion
  7.3 0.0 copy-start.4
  7.3 0.1 multiply_reduce_fusion
  7.5 0.0 copy-done.7
  7.5 0.6 select_n.76.slot_ref
  8.1 0.0 copy-done.1
  8.1 0.9 copy.46.wq_ref
  9.1 0.0 copy-done.2
  9.1 0.0 copy-start.5
  9.1 0.9 copy.47.wk_ref
  10.0 0.0 copy-done.3
  10.0 0.0 copy-start.6
  10.0 0.9 copy.48.wv_ref
  10.9 0.0 copy-done.4
  10.9 0.9 copy.49.wq_cross_ref
  11.8 0.0 copy-done.5
  11.8 0.9 copy.50.wk_cross_ref
  12.8 0.0 copy-done.6
  12.8 0.9 copy.51.wv_cross_ref
  13.7 0.0 copy-start
  13.7 54.7 %attention_front.1.own_ref = bf16[2,256,768]{2,1,0:T(8,128)(2,1)} custom-call(bf16[8,256,768]{2,1,0:T(8,128)(2,1)} %dec_ref.1, bf16[8,128,768]{2,1,0:T(8,128)(2,1)} %enc_ref.1, s32[8,128]{1,0:T(8,128)} %pad_ref.1, f32[3,256,256]{2,1,0:T(8,128)} %bias_ref.1, f32[1,768]{1,0:T(1,128)} %broadcast_in_dim.14.gain_self_ref, ...), custom_call_target="tpu_custom_call" | custom-call | tf_op jit(solution)/shard_map/attention_front/pallas_call | solution.py:530
  68.3 0.0 copy-done
  68.4 0.2 copy.64
  68.5 0.1 fusion.20
  68.6 0.9 fusion.19.route_ref
  69.5 0.4 copy.66
  69.9 0.4 copy.54
  70.3 3.0 %fusion.8.code_ref = s32[2048,1]{1,0:T(8,128)} fusion(s32[2048,1]{1,0:T(8,128)S(1)} %copy.54, s32[1,2048]{0,1:T(8,128)S(1)} %copy.66), kind=kLoop, calls=%fused_computation.23 | loop fusion | flops 94208 | bytes 24576 | tf_op jit(solution)/shard_map/jit(_where)/select_n | solution.py:582
  73.3 89.7 %expert_exchange.1 = bf16[2048,768]{1,0:T(8,128)(2,1)} custom-call(bf16[2,256,768]{2,1,0:T(8,128)(2,1)} %attention_front.1.own_ref, s32[8,1,256]{2,1,0:T(1,128)} %select_n.76.slot_ref, s32[2048,1]{1,0:T(8,128)} %fusion.8.code_ref, f32[1,768]{1,0:T(1,128)} %broadcast_in_dim.16.gain_ref, bf16[768,384]{1,0:T(8,128)(2,1)} %fusion.19.route_ref, ...), custom_call_target="tpu_custom_call" | custom-call | tf_op jit(solution)/shard_map/expert_exchange/pallas_call | solution.py:262
  163.0 3.8 %copy.68 = bf16[8,256,768]{2,1,0:T(8,128)(2,1)} copy(bf16[8,256,768]{2,1,0:T(8,128)(2,1)} %bitcast.27) | data formatting | bytes 6291456
  (4 shorter events, 0.1 us)
Async XLA Ops:
  6.1 1.4 copy-start.7
  6.3 1.8 %copy-start.1 = (bf16[768,192]{0,1:T(8,128)(2,1)S(1)}, bf16[768,192]{0,1:T(8,128)(2,1)}, u32[]{:S(2)}) copy-start(bf16[768,192]{0,1:T(8,128)(2,1)} %param.25) | copy-start | bytes 884740
  6.7 2.4 %copy-start.2 = (bf16[768,192]{0,1:T(8,128)(2,1)S(1)}, bf16[768,192]{0,1:T(8,128)(2,1)}, u32[]{:S(2)}) copy-start(bf16[768,192]{0,1:T(8,128)(2,1)} %param.26) | copy-start | bytes 884740
  7.0 2.9 %copy-start.3 = (bf16[768,192]{0,1:T(8,128)(2,1)S(1)}, bf16[768,192]{0,1:T(8,128)(2,1)}, u32[]{:S(2)}) copy-start(bf16[768,192]{0,1:T(8,128)(2,1)} %param.27) | copy-start | bytes 884740
  7.3 3.6 %copy-start.4 = (bf16[768,192]{0,1:T(8,128)(2,1)S(1)}, bf16[768,192]{0,1:T(8,128)(2,1)}, u32[]{:S(2)}) copy-start(bf16[768,192]{0,1:T(8,128)(2,1)} %param.30) | copy-start | bytes 884740
  9.1 2.8 %copy-start.5 = (bf16[768,192]{0,1:T(8,128)(2,1)S(1)}, bf16[768,192]{0,1:T(8,128)(2,1)}, u32[]{:S(2)}) copy-start(bf16[768,192]{0,1:T(8,128)(2,1)} %param.31) | copy-start | bytes 884740
  10.0 2.8 %copy-start.6 = (bf16[768,192]{0,1:T(8,128)(2,1)S(1)}, bf16[768,192]{0,1:T(8,128)(2,1)}, u32[]{:S(2)}) copy-start(bf16[768,192]{0,1:T(8,128)(2,1)} %param.32) | copy-start | bytes 884740
  13.7 54.7 %copy-start = (f32[768,32]{0,1:T(8,128)S(1)}, f32[768,32]{0,1:T(8,128)}, u32[]{:S(2)}) copy-start(f32[768,32]{0,1:T(8,128)} %param.35) | copy-start | bytes 294916
